TPU v7x, 32 devices: a whole 2x2x4 slice. The times are simulated.
32 devices in a mesh: batch: 2 (over x), tp: 4 (over z), sp: 4 (over y, core).
Axes of the slice: x: 2, y: 2, z: 4, core: 2. Of those that a mesh axis runs over, the one named last changes fastest.
Arguments:
- tokens: bfloat16 [16384, 1024], P(('batch', 'sp')), parts along dimension 0
- glob_pos: int32 [1024], P('batch'), parts along dimension 0
- rel_bias: float32 [16, 513], P('tp')
- w_query: bfloat16 [1024, 1024], P(None, 'tp')
- w_key: bfloat16 [1024, 1024], P(None, 'tp')
- w_value: bfloat16 [1024, 1024], P(None, 'tp')
- w_query_glob: bfloat16 [1024, 1024], P(None, 'tp')
- w_out: bfloat16 [1024, 1024], P('tp')
- w_up: bfloat16 [1024, 4096], P(None, 'tp')
- w_down: bfloat16 [4096, 1024], P('tp')
Outputs:
- output: bfloat16 [16384, 1024], P(('batch', 'sp')), parts along dimension 0
There are 2 independent parts. A program takes and returns all parts, laid end to end along the dimension named above; an argument that names none is the same for every part.
All inputs are finite; a program needn't handle non-finite values.
Results may differ from a plain program's by a relative error of at most 0.0116152.
Values are sent between devices in bfloat16 or wider.
A program may use at most 1 GiB of HBM per device.

v0:
```python
import jax
import jax.numpy as jnp
from jax import lax
from jax.sharding import PartitionSpec as P


def solution(mesh):
    n_seq = mesh.shape["sp"]
    to_right = [(sender, sender + 1) for sender in range(n_seq - 1)]
    to_left = [(sender + 1, sender) for sender in range(n_seq - 1)]

    def local_layer(tokens, glob_pos, rel_bias, w_query, w_key, w_value, w_query_glob, w_out, w_up, w_down):
        local_rows = tokens.shape[0]
        local_heads = rel_bias.shape[0]
        window = (rel_bias.shape[1] - 1) // 2
        local_dim = w_query.shape[1]
        head_dim = local_dim // local_heads
        num_glob = glob_pos.shape[0]
        n_blocks = local_rows // window
        seq_len = local_rows * n_seq
        score_scale = head_dim ** -0.5
        row_start = lax.axis_index("sp") * local_rows
        heads_shape = (local_rows, local_heads, head_dim)
        glob_shape = (num_glob, local_heads, head_dim)

        def project(weight):
            return jnp.dot(tokens, weight, preferred_element_type=jnp.float32).astype(jnp.bfloat16)

        q_flat = project(w_query)
        k_flat = project(w_key)
        v_flat = project(w_value)
        local_slot = glob_pos - row_start
        is_owned = (local_slot >= 0) & (local_slot < local_rows)
        safe_slot = jnp.clip(local_slot, 0, local_rows - 1)
        zero_half = jnp.zeros((), jnp.bfloat16)

        def pick_rows(source):
            return jnp.where(is_owned[:, None], jnp.take(source, safe_slot, axis=0), zero_half)

        qg_part = jnp.dot(pick_rows(tokens), w_query_glob, preferred_element_type=jnp.float32).astype(jnp.bfloat16)
        glob_rows = lax.psum(jnp.stack([qg_part, pick_rows(k_flat), pick_rows(v_flat)]), "sp")
        glob_q = glob_rows[0].reshape(glob_shape)
        glob_k = glob_rows[1].reshape(glob_shape)
        glob_v = glob_rows[2].reshape(glob_shape)

        kv_loc = jnp.stack([k_flat, v_flat]).reshape((2,) + heads_shape)
        left_halo = lax.ppermute(kv_loc[:, local_rows - window:], "sp", to_right)
        right_halo = lax.ppermute(kv_loc[:, :window], "sp", to_left)
        kv_ext = jnp.concatenate([left_halo, kv_loc, right_halo], axis=1)
        kv_blocks = kv_ext.reshape(2, n_blocks + 2, window, local_heads, head_dim)
        kv_win = jnp.concatenate([kv_blocks[:, :-2], kv_blocks[:, 1:-1], kv_blocks[:, 2:]], axis=2)
        q_blocks = q_flat.reshape(n_blocks, window, local_heads, head_dim)

        rel_offs = jnp.arange(3 * window)[None, :] - jnp.arange(window)[:, None]
        in_band = (rel_offs >= 0) & (rel_offs <= 2 * window)
        band_bias = jnp.take(rel_bias, jnp.clip(rel_offs, 0, 2 * window), axis=1)
        blk_start = row_start + jnp.arange(n_blocks) * window
        key_pos = blk_start[:, None] - window + jnp.arange(3 * window)[None, :]
        key_ok = (key_pos >= 0) & (key_pos < seq_len)
        win_mask = in_band[None, None] & key_ok[:, None, None, :]
        win_scores = jnp.einsum("cqhd,ckhd->chqk", q_blocks, kv_win[0], preferred_element_type=jnp.float32)
        win_scores = jnp.where(win_mask, win_scores * score_scale + band_bias, -jnp.inf)
        query_pos = blk_start[:, None] + jnp.arange(window)[None, :]
        far_mask = jnp.abs(query_pos[:, :, None] - glob_pos[None, None, :]) > window
        glob_scores = jnp.einsum("cqhd,ghd->chqg", q_blocks, glob_k, preferred_element_type=jnp.float32)
        glob_scores = jnp.where(far_mask[:, None], glob_scores * score_scale, -jnp.inf)
        row_max = jnp.maximum(win_scores.max(axis=-1), glob_scores.max(axis=-1))[..., None]
        win_exp = jnp.exp(win_scores - row_max)
        glob_exp = jnp.exp(glob_scores - row_max)
        soft_sum = win_exp.sum(axis=-1, keepdims=True) + glob_exp.sum(axis=-1, keepdims=True)
        win_out = jnp.einsum("chqk,ckhd->cqhd", (win_exp / soft_sum).astype(jnp.bfloat16), kv_win[1], preferred_element_type=jnp.float32)
        win_out = win_out + jnp.einsum("chqg,ghd->cqhd", (glob_exp / soft_sum).astype(jnp.bfloat16), glob_v, preferred_element_type=jnp.float32)
        win_out = win_out.astype(jnp.bfloat16).reshape(heads_shape)

        part_scores = jnp.einsum("ghd,rhd->hgr", glob_q, kv_loc[0], preferred_element_type=jnp.float32) * score_scale
        part_max = part_scores.max(axis=-1)
        part_exp = jnp.exp(part_scores - part_max[..., None])
        part_sum = part_exp.sum(axis=-1)
        part_out = jnp.einsum("hgr,rhd->ghd", part_exp.astype(jnp.bfloat16), kv_loc[1], preferred_element_type=jnp.float32)
        glob_max = lax.pmax(part_max, "sp")
        rescale = jnp.exp(part_max - glob_max)
        tot_sum, tot_out = lax.psum((part_sum * rescale, part_out * rescale.T[:, :, None]), "sp")
        glob_out = (tot_out / tot_sum.T[:, :, None]).astype(jnp.bfloat16)
        slot_rows = jnp.where(is_owned, local_slot, local_rows)
        heads_out = win_out.at[slot_rows].set(glob_out, mode="drop")

        attn_part = jnp.dot(heads_out.reshape(local_rows, local_dim), w_out, preferred_element_type=jnp.float32)
        attn_proj = lax.psum(attn_part, "tp")
        hidden = (tokens.astype(jnp.float32) + attn_proj).astype(jnp.bfloat16)
        act_vals = jax.nn.gelu(jnp.dot(hidden, w_up, preferred_element_type=jnp.float32)).astype(jnp.bfloat16)
        mlp_out = lax.psum(jnp.dot(act_vals, w_down, preferred_element_type=jnp.float32), "tp")
        return (hidden.astype(jnp.float32) + mlp_out).astype(jnp.bfloat16)

    row_spec = P(("batch", "sp"), None)
    col_spec = P(None, "tp")
    head_spec = P("tp", None)
    in_specs = (row_spec, P("batch"), head_spec, col_spec, col_spec, col_spec, col_spec, head_spec, col_spec, head_spec)
    return jax.shard_map(local_layer, mesh=mesh, in_specs=in_specs, out_specs=row_spec, check_vma=False)
```

profile of v0, /device:TPU:0, one launch (start us, length us, event | category | flops | bytes accessed | tf_op | source)
XLA Modules:
  0.0 1648.6 jit_solution(8902402338503437686)
XLA Ops:
  11.6 6.2 gather_fusion.1
  20.8 4.6 convolution_convert_fusion.1
  53.6 712.3 %gather_fusion = f32[196608,4]{1,0:T(8,128)} fusion(f32[4,513]{0,1:T(8,128)S(1)} %copy.93, s32[196608]{0:T(1024)} %broadcast_clamp_fusion), kind=kCustom, calls=%fused_computation.2 | custom fusion | bytes 7077888 | tf_op jit(solution)/shard_map/jit(_take)/gather | solution.py:56
  765.9 56.1 %copy.94 = f32[256,768,4]{1,0,2:T(8,128)} copy(f32[256,768,4]{2,1,0:T(8,128)} %bitcast.4) | data formatting | bytes 6291456 | tf_op jit(solution)/shard_map/jit(_take)/gather | solution.py:56
  838.4 6.3 reshape.167
  844.7 5.3 fusion.65
  854.3 14.7 fusion.1
  873.7 11.6 fusion.5
  885.4 8.6 fusion.2
  895.1 8.0 fusion
  903.2 10.0 fusion.15
  914.3 8.1 multiply_reduce_fusion
  922.4 7.7 pmax.7
  930.1 8.0 fusion.3
  940.7 5.3 fusion.30
  946.1 15.5 fusion.26
  964.1 6.2 psum.37
  970.3 10.5 all-reduce.7.cloned.1.call-done
  982.2 47.7 %scatter_fusion = bf16[2048,4,64]{2,1,0:T(4,128)(2,1)} fusion(bf16[2048,4,64]{2,1,0:T(4,128)(2,1)} %bitcast.93, s32[512]{0:T(512)S(1)} %compare_select_fusion.2, bf16[512,4,64]{2,1,0:T(4,128)(2,1)S(1)} %copy.108), kind=kCustom, calls=%fused_computation.4 | custom fusion | bytes 788480 | tf_op jit(solution)/shard_map/scatter | solution.py:85
  1032.8 5.6 fusion.67
  1038.5 288.6 %all-reduce.9.cloned.1.call-done = f32[2048,1024]{1,0:T(8,128)} async-done(((f32[2048,1024]{1,0:T(8,128)}), f32[2048,1024]{1,0:T(8,128)}) %all-reduce.9.cloned.1.call-update) | async-done | bytes 8388624 | tf_op jit(solution)/shard_map/psum | solution.py:88
  1327.1 15.0 fusion.19
  1342.1 287.9 %all-reduce.11.cloned.1.call-done = f32[2048,1024]{1,0:T(8,128)} async-done(((f32[2048,1024]{1,0:T(8,128)}), f32[2048,1024]{1,0:T(8,128)}) %all-reduce.11.cloned.1.call-update) | async-done | bytes 8388624 | tf_op jit(solution)/shard_map/psum | solution.py:91
  1630.0 11.5 add_convert_fusion
  (94 shorter events, 73.1 us)
Async XLA Ops:
  6.5 1320.6 %copy-start = (bf16[1024,1024]{1,0:T(8,128)(2,1)S(1)}, bf16[1024,1024]{1,0:T(8,128)(2,1)}, u32[]{:S(2)}) copy-start(bf16[1024,1024]{1,0:T(8,128)(2,1)} %param.21) | copy-start | bytes 6291460
  6.5 5.1 copy-start.10
  6.5 862.5 %all-reduce.5.cloned.1.call-start = ((), (), s32[]{:S(2)}) async-start(), calls=%async_computation | async-start | bytes 1572864 | tf_op jit(solution)/shard_map/psum | solution.py:41
  32.3 16.9 %copy-start.11 = (f32[4,513]{1,0:T(4,128)S(1)}, f32[4,513]{1,0:T(4,128)}, u32[]{:S(2)}) copy-start(f32[4,513]{1,0:T(4,128)} %param.14) | copy-start | bytes 24628
  35.2 945.6 %all-reduce.7.cloned.1.call-start = ((), (), s32[]{:S(2)}) async-start(), calls=%async_computation.1 | async-start | bytes 1048576 | tf_op jit(solution)/shard_map/psum | solution.py:82
  37.1 798.5 %collective-permute-start.1 = (bf16[2,256,4,64]{1,3,2,0:T(8,128)(2,1)}, bf16[2,256,4,64]{1,3,2,0:T(8,128)(2,1)}, u32[]{:S(2)}, u32[]{:S(2)}) collective-permute-start(bf16[2,256,4,64]{1,3,2,0:T(8,128)(2,1)} %get-tuple-element.12), channel_id=1, source_target_pairs={{1,0},{2,1},{3,2},{5,4},{6,5},{7,6},{9,8},{10,9},{11,10},{13,12},{... | collective-permute-start | bytes 786440 | tf_op jit(solution)/shard_map/ppermute | solution.py:48
  38.4 797.2 %collective-permute-start = (bf16[2,256,4,64]{1,3,2,0:T(8,128)(2,1)}, bf16[2,256,4,64]{1,3,2,0:T(8,128)(2,1)}, u32[]{:S(2)}, u32[]{:S(2)}) collective-permute-start(bf16[2,256,4,64]{1,3,2,0:T(8,128)(2,1)} %get-tuple-element.11), channel_id=1, source_target_pairs={{0,1},{1,2},{2,3},{4,5},{5,6},{6,7},{8,9},{9,10},{10,11},{12,13},{... | collective-permute-start | bytes 786440 | tf_op jit(solution)/shard_map/ppermute | solution.py:47
  765.9 56.2 %copy-start.7 = (pred[256,768]{1,0:T(8,128)(4,1)S(1)}, pred[256,768]{1,0:T(8,128)(4,1)}, u32[]{:S(2)}) copy-start(pred[256,768]{1,0:T(8,128)(4,1)} %fusion.45) | copy-start | bytes 589828
  850.1 4.2 copy-start.2
  850.1 4.2 copy-start.4
  851.6 2.7 copy-start.8
  873.7 11.7 copy-start.6
  873.7 20.4 %slice-start = ((s8[25165824]{0:T(1024)(128)(4,1)}), s8[4194304]{0:T(1024)(128)(4,1)S(1)}, s32[]{:S(2)}) async-start(s8[25165824]{0:T(1024)(128)(4,1)} %bitcast.85), calls=%async_computation.4 | async-start | bytes 8388608
  873.7 20.4 %slice-start.1 = ((s8[25165824]{0:T(1024)(128)(4,1)}), s8[4194304]{0:T(1024)(128)(4,1)S(1)}, s32[]{:S(2)}) async-start(s8[25165824]{0:T(1024)(128)(4,1)} %bitcast.85), calls=%async_computation.5 | async-start | bytes 8388608
  873.7 20.4 %slice-start.2 = ((s8[25165824]{0:T(1024)(128)(4,1)}), s8[4194304]{0:T(1024)(128)(4,1)S(1)}, s32[]{:S(2)}) async-start(s8[25165824]{0:T(1024)(128)(4,1)} %bitcast.85), calls=%async_computation.6 | async-start | bytes 8388608
  873.7 20.4 %slice-start.3 = ((s8[25165824]{0:T(1024)(128)(4,1)}), s8[4194304]{0:T(1024)(128)(4,1)S(1)}, s32[]{:S(2)}) async-start(s8[25165824]{0:T(1024)(128)(4,1)} %bitcast.85), calls=%async_computation.7 | async-start | bytes 8388608
  885.3 8.7 slice-start.4
  885.3 9.8 slice-start.5
  885.4 9.8 copy-start.3
  885.4 9.8 copy-start.5
  895.1 8.1 copy-start.9
  930.1 10.6 copy-start.1
  946.1 381.0 %all-reduce.9.cloned.1.call-start = ((), (), s32[]{:S(2)}) async-start(), calls=%async_computation.2 | async-start | bytes 16777216 | tf_op jit(solution)/shard_map/psum | solution.py:88
  1038.4 591.6 %all-reduce.11.cloned.1.call-start = ((), (), s32[]{:S(2)}) async-start(), calls=%async_computation.3 | async-start | bytes 16777216 | tf_op jit(solution)/shard_map/psum | solution.py:91
Sparse Core Ops, SparseCore 0:
  35.3 38.9 all-reduce.4
  946.2 34.5 all-reduce.6
  1038.5 288.5 all-reduce.8
  1342.2 287.7 all-reduce.10
where the time goes:
time: 1670 us; the launch traced here: 1650 us
  local copies, waits for them, and re-layouts  870 us (52%)
  waiting for transfers between devices  587 us (35%)
  matrix products  101 us (6%)
  other arithmetic  57.7 us (3%)
    gather x2, local copies, waits for them, and re-layouts, local_layer(): band_bias = jnp.take(rel_bias, jnp.clip(rel_offs, 0, 2 * window), axis=1)  768 us
    psum x1, waiting for transfers between devices, local_layer(): attn_proj = lax.psum(attn_part, 'tp')  289 us
    psum x1, waiting for transfers between devices, local_layer(): lax.psum(jnp.dot(act_vals, w_down, preferred_element_type=jnp.float32), '...  288 us
    scatter x2, local copies, waits for them, and re-layouts, local_layer(): heads_out = win_out.at[slot_rows].set(glob_out, mode='drop')  50.6 us
  transfers between devices with their start and end apart: 6, of which 3 were waited for; matrix products, arithmetic and copies ran while one was open for 51% of the time, Pallas kernels for 0%

commit v1 on v0

v1 whole, which is shorter than its diff:
```python
import functools

import jax
import jax.numpy as jnp
from jax import lax
from jax.experimental import pallas as pl
from jax.experimental.pallas import tpu as pltpu
from jax.sharding import PartitionSpec as P

BLK = 256
F32 = jnp.float32
BF16 = jnp.bfloat16
VMEM_CAP = 60 * 1024 * 1024


def dot_nn(a, b):
    return lax.dot_general(a, b, (((1,), (0,)), ((), ())), preferred_element_type=F32)


def dot_nt(a, b):
    return lax.dot_general(a, b, (((1,), (1,)), ((), ())), preferred_element_type=F32)


def whole(shape):
    return pl.BlockSpec(shape, lambda *_: (0,) * len(shape), pipeline_mode=pl.Buffered(1))


def head_masked(x, head_dim, odd):
    lane = lax.broadcasted_iota(jnp.int32, x.shape, 1)
    keep = (lane >= head_dim) if odd else (lane < head_dim)
    return jnp.where(keep, x, jnp.zeros_like(x))


def project_kernel(scale, slot_ref, x_ref, wq_ref, wk_ref, wv_ref, wg_ref, q_ref, k_ref, v_ref, sel_ref, acc_ref):
    i = pl.program_id(0)
    x = x_ref[...]
    width = wq_ref.shape[1]
    q_ref[...] = dot_nn(x, wq_ref[...]).astype(BF16) * scale
    k = dot_nn(x, wk_ref[...]).astype(BF16)
    v = dot_nn(x, wv_ref[...]).astype(BF16)
    qg = dot_nn(x, wg_ref[...]).astype(BF16) * scale
    k_ref[...] = k
    v_ref[...] = v
    cols = lax.broadcasted_iota(jnp.int32, (slot_ref.shape[0], x.shape[0]), 1) + i * x.shape[0]
    pick = jnp.where(slot_ref[...] == cols, 1.0, 0.0).astype(BF16)

    @pl.when(i == 0)
    def _():
        acc_ref[...] = jnp.zeros_like(acc_ref)

    acc_ref[:, :width] += dot_nn(pick, qg)
    acc_ref[:, width:2 * width] += dot_nn(pick, k)
    acc_ref[:, 2 * width:] += dot_nn(pick, v)

    @pl.when(i == pl.num_programs(0) - 1)
    def _():
        sel_ref[...] = acc_ref[...].astype(BF16)


def project(x, slot_col, wq, wk, wv, wg, scale):
    rows, dim = x.shape
    width = wq.shape[1]
    num_glob = slot_col.shape[0]
    row_block = pl.BlockSpec((BLK, width), lambda i: (i, 0))
    return pl.pallas_call(
        functools.partial(project_kernel, scale),
        grid=(rows // BLK,),
        in_specs=[whole((num_glob, 1)), pl.BlockSpec((BLK, dim), lambda i: (i, 0))] + [whole((dim, width))] * 4,
        out_specs=[row_block, row_block, row_block, pl.BlockSpec((num_glob, 3 * width), lambda i: (0, 0))],
        out_shape=[jax.ShapeDtypeStruct((rows, width), BF16)] * 3 + [jax.ShapeDtypeStruct((num_glob, 3 * width), BF16)],
        scratch_shapes=[pltpu.VMEM((num_glob, 3 * width), F32)],
        compiler_params=pltpu.CompilerParams(vmem_limit_bytes=VMEM_CAP),
        cost_estimate=pl.CostEstimate(flops=2 * rows * dim * width * 4, bytes_accessed=2 * rows * dim * 2, transcendentals=0),
        name="project",
    )(slot_col, x, wq, wk, wv, wg)


def glob_kernel(head_dim, qg_ref, k_ref, v_ref, out_ref, stat_ref):
    k = k_ref[...]
    v = v_ref[...]
    qg = qg_ref[...]
    outs, stats = [], []
    for odd in (False, True):
        s = dot_nt(head_masked(qg, head_dim, odd), k)
        m = jnp.max(s, axis=1, keepdims=True)
        p = jnp.exp(s - m)
        stats.append((m, jnp.sum(p, axis=1, keepdims=True)))
        outs.append(dot_nn(p.astype(BF16), v))
    lane = lax.broadcasted_iota(jnp.int32, out_ref.shape, 1)
    out_ref[...] = jnp.where(lane < head_dim, outs[0], outs[1])
    (m0, l0), (m1, l1) = stats
    stat_ref[...] = jnp.where(lane == 0, m0, jnp.where(lane == 1, m1, jnp.where(lane == 2, l0, l1)))


def glob_partial(sel, k, v, head_dim):
    rows, width = k.shape
    num_glob = sel.shape[0]
    pair = 2 * head_dim
    tile = 128
    kv_spec = pl.BlockSpec((rows, pair), lambda p, i: (0, p))
    out_spec = pl.BlockSpec((tile, pair), lambda p, i: (i, p))
    return pl.pallas_call(
        functools.partial(glob_kernel, head_dim),
        grid=(width // pair, num_glob // tile),
        in_specs=[out_spec, kv_spec, kv_spec],
        out_specs=[out_spec, out_spec],
        out_shape=[jax.ShapeDtypeStruct((num_glob, width), F32)] * 2,
        compiler_params=pltpu.CompilerParams(vmem_limit_bytes=VMEM_CAP),
        cost_estimate=pl.CostEstimate(flops=4 * num_glob * rows * width, bytes_accessed=4 * rows * width, transcendentals=0),
        name="glob_partial",
    )(sel, k, v)


def window_kernel(window, head_dim, blk0, n_blocks, edge_ref, bias_ref, slot_ref, q_ref, kx_ref, vx_ref, sel_ref, gout_ref, o_ref, band_ref):
    step = pl.program_id(0)
    blk = step + blk0
    heads, span = bias_ref.shape[0], bias_ref.shape[2]
    width = 3 * window
    pair = 2 * head_dim
    cols = lax.broadcasted_iota(jnp.int32, (BLK, width), 1)
    cut_left = (blk == 0) & (edge_ref[0] == 1)
    cut_right = (blk == n_blocks - 1) & (edge_ref[1] == 1)

    @pl.when((step == 0) | (blk == 1) | (blk == n_blocks - 1))
    def _():
        lo = jnp.where(cut_left, window, 0)
        hi = jnp.where(cut_right, 2 * window, width)
        for h in range(heads):
            row = jnp.broadcast_to(bias_ref[h], (BLK, span))
            band = pltpu.roll(row, 0, 1, stride=1, stride_axis=0)[:, :width]
            band_ref[h] = jnp.where((cols >= lo) & (cols < hi), band, -jnp.inf)

    slot = slot_ref[...]
    dist = slot - blk * BLK - lax.broadcasted_iota(jnp.int32, (BLK, slot.shape[1]), 0)
    near = jnp.abs(dist) <= window
    pick = jnp.where(dist == 0, 1.0, 0.0)
    is_glob = jnp.max(pick, axis=1, keepdims=True) > 0.0
    pick = pick.astype(BF16)
    start = pl.multiple_of(step * BLK, BLK)
    lane = lax.broadcasted_iota(jnp.int32, (BLK, pair), 1)
    gwidth = gout_ref.shape[1]
    for p in range(heads // 2):
        at = slice(p * pair, (p + 1) * pair)
        q = q_ref[:, at]
        k_win = kx_ref[pl.ds(start, width), at]
        v_win = vx_ref[pl.ds(start, width), at]
        k_glob = sel_ref[:, gwidth + p * pair:gwidth + (p + 1) * pair]
        v_glob = sel_ref[:, 2 * gwidth + p * pair:2 * gwidth + (p + 1) * pair]
        outs = []
        for odd in (False, True):
            qh = head_masked(q, head_dim, odd)
            s_win = dot_nt(qh, k_win) + band_ref[2 * p + int(odd)]
            s_glob = jnp.where(near, -jnp.inf, dot_nt(qh, k_glob))
            m = jnp.maximum(jnp.max(s_win, axis=1, keepdims=True), jnp.max(s_glob, axis=1, keepdims=True))
            e_win = jnp.exp(s_win - m)
            e_glob = jnp.exp(s_glob - m)
            total = jnp.sum(e_win, axis=1, keepdims=True) + jnp.sum(e_glob, axis=1, keepdims=True)
            inv = 1.0 / total
            o = dot_nn((e_win * inv).astype(BF16), v_win)
            outs.append(o + dot_nn((e_glob * inv).astype(BF16), v_glob))
        o = jnp.where(lane < head_dim, outs[0], outs[1])
        ins = dot_nn(pick, gout_ref[:, at])
        o_ref[:, at] = jnp.where(is_glob, ins, o).astype(BF16)


def window_attn(edge, bias, slot_row, q, kx, vx, sel, gout, window, head_dim, chunk, n_chunks):
    rows, width = q.shape
    blocks = rows // BLK
    per = blocks // n_chunks
    num_glob = sel.shape[0]
    heads, _, span = bias.shape
    ext = per * BLK + 2 * window
    kx = lax.slice_in_dim(kx, chunk * per * BLK, chunk * per * BLK + ext)
    vx = lax.slice_in_dim(vx, chunk * per * BLK, chunk * per * BLK + ext)
    return pl.pallas_call(
        functools.partial(window_kernel, window, head_dim, chunk * per, blocks),
        grid=(per,),
        in_specs=[
            pl.BlockSpec(memory_space=pltpu.SMEM),
            whole((heads, 1, span)),
            whole((1, num_glob)),
            pl.BlockSpec((BLK, width), lambda i: (chunk * per + i, 0)),
            whole((ext, width)),
            whole((ext, width)),
            whole((num_glob, 3 * width)),
            whole((num_glob, width)),
        ],
        out_specs=pl.BlockSpec((BLK, width), lambda i: (i, 0)),
        out_shape=jax.ShapeDtypeStruct((per * BLK, width), BF16),
        scratch_shapes=[pltpu.VMEM((heads, BLK, 3 * window), F32)],
        compiler_params=pltpu.CompilerParams(vmem_limit_bytes=VMEM_CAP),
        cost_estimate=pl.CostEstimate(flops=4 * per * BLK * (3 * window + num_glob) * width, bytes_accessed=8 * rows * width, transcendentals=0),
        name="window_attn",
    )(edge, bias, slot_row, q, kx, vx, sel, gout)


def mlp_kernel(n_tp, o_ref, x_ref, wo_ref, wu_ref, wd_ref, out_ref):
    dim = x_ref.shape[1]
    shard = o_ref.shape[2]
    acc = x_ref[...].astype(F32)
    for t in range(n_tp):
        acc += dot_nn(o_ref[t], wo_ref[:, t].reshape(shard, dim))
    hidden = acc.astype(BF16)
    acc = hidden.astype(F32)
    for t in range(n_tp):
        up = dot_nn(hidden, wu_ref[:, t].reshape(dim, -1))
        act = jax.nn.gelu(up).astype(BF16)
        acc += dot_nn(act, wd_ref[:, t].reshape(-1, dim))
    out_ref[...] = acc.astype(BF16)


def mlp(o_all, x, packed, chunk):
    n_tp, rows, shard = o_all.shape
    dim = x.shape[1]
    nb, _, ns, _, _ = packed.shape
    up_rows = dim // (nb * ns)
    out_rows = shard // (nb * ns)
    tile = 256
    first = chunk * (rows // tile)
    big = (nb, n_tp, ns, up_rows, dim)
    return pl.pallas_call(
        functools.partial(mlp_kernel, n_tp),
        grid=(rows // tile,),
        in_specs=[
            pl.BlockSpec((n_tp, tile, shard), lambda i: (0, i, 0)),
            pl.BlockSpec((tile, dim), lambda i: (first + i, 0)),
            pl.BlockSpec((nb, n_tp, ns, out_rows, dim), lambda i: (0, 0, 0, 2 * up_rows // out_rows, 0), pipeline_mode=pl.Buffered(1)),
            pl.BlockSpec(big, lambda i: (0, 0, 0, 0, 0), pipeline_mode=pl.Buffered(1)),
            pl.BlockSpec(big, lambda i: (0, 0, 0, 1, 0), pipeline_mode=pl.Buffered(1)),
        ],
        out_specs=pl.BlockSpec((tile, dim), lambda i: (i, 0)),
        out_shape=jax.ShapeDtypeStruct((rows, dim), BF16),
        compiler_params=pltpu.CompilerParams(vmem_limit_bytes=VMEM_CAP),
        cost_estimate=pl.CostEstimate(flops=2 * rows * dim * dim * 9, bytes_accessed=4 * rows * dim, transcendentals=0),
        name="mlp",
    )(o_all, x, packed, packed, packed)


def solution(mesh):
    n_seq = mesh.shape["sp"]
    n_tp = mesh.shape["tp"]
    n_batch = mesh.shape["batch"]
    to_right = [(sender, sender + 1) for sender in range(n_seq - 1)]
    to_left = [(sender + 1, sender) for sender in range(n_seq - 1)]

    def local_layer(tokens, glob_pos, rel_bias, w_query, w_key, w_value, w_query_glob, w_out, w_up, w_down):
        rows, dim = tokens.shape
        heads = rel_bias.shape[0]
        window = (rel_bias.shape[1] - 1) // 2
        width = w_query.shape[1]
        head_dim = width // heads
        num_glob = glob_pos.shape[0]
        sp = lax.axis_index("sp")
        slot = glob_pos - sp * rows

        replica = lax.axis_index("batch") * n_seq + sp
        n_rep = n_batch * n_seq

        def my_rows(weight):
            size = weight.shape[0] // n_rep
            return lax.dynamic_slice_in_dim(weight, replica * size, size)

        piece = jnp.concatenate([my_rows(w_up), my_rows(w_down), my_rows(w_out)])
        packed = lax.all_gather(piece, ("batch", "tp", "sp"), axis=0, tiled=False)
        packed = packed.reshape(n_batch, n_tp, n_seq, *piece.shape)

        q, k, v, sel = project(tokens, slot[:, None], w_query, w_key, w_value, w_query_glob, head_dim ** -0.5)

        def spread(part):
            return lax.all_to_all(part, "sp", 0, 0)

        share = num_glob // n_seq
        got = spread(sel.reshape(n_seq, share, 3 * width))
        mine = got.astype(F32).sum(axis=0).astype(BF16)
        sel = spread(jnp.broadcast_to(mine[None], (n_seq,) + mine.shape)).reshape(num_glob, 3 * width)

        kv = jnp.stack([k, v])
        left = lax.ppermute(kv[:, rows - window:], "sp", to_right)
        right = lax.ppermute(kv[:, :window], "sp", to_left)
        kx = jnp.concatenate([left[0], k, right[0]])
        vx = jnp.concatenate([left[1], v, right[1]])

        part_out, part_stat = glob_partial(sel, k, v, head_dim)
        got_out = spread(part_out.reshape(n_seq, share, width))
        stat = part_stat.reshape(num_glob, heads // 2, 2 * head_dim)[:, :, :4]
        got_stat = spread(stat.reshape(n_seq, share, heads // 2, 2, 2))
        part_max = got_stat[:, :, :, 0].reshape(n_seq, share, heads)
        part_sum = got_stat[:, :, :, 1].reshape(n_seq, share, heads)
        rescale = jnp.exp(part_max - part_max.max(axis=0))
        inv = 1.0 / (part_sum * rescale).sum(axis=0)
        merged = (got_out.reshape(n_seq, share, heads, head_dim) * rescale[..., None]).sum(axis=0) * inv[..., None]
        merged = merged.astype(BF16).reshape(share, width)
        gout = spread(jnp.broadcast_to(merged[None], (n_seq,) + merged.shape)).reshape(num_glob, width)

        span = 4 * window
        bias = jnp.pad(rel_bias, ((0, 0), (0, span - rel_bias.shape[1])), constant_values=-jnp.inf)[:, None]
        edge = jnp.stack([sp == 0, sp == n_seq - 1]).astype(jnp.int32)
        n_chunks = 4
        outs = []
        for c in range(n_chunks):
            o = window_attn(edge, bias, slot[None], q, kx, vx, sel, gout, window, head_dim, c, n_chunks)
            o_all = lax.all_gather(o, "tp", axis=0)
            outs.append(mlp(o_all, tokens, packed, c))
        return jnp.concatenate(outs)

    row_spec = P(("batch", "sp"), None)
    col_spec = P(None, "tp")
    head_spec = P("tp", None)
    in_specs = (row_spec, P("batch"), head_spec, col_spec, col_spec, col_spec, col_spec, head_spec, col_spec, head_spec)
    return jax.shard_map(local_layer, mesh=mesh, in_specs=in_specs, out_specs=row_spec, check_vma=False)
```

time: 1670 us -> 387 us (0.23)
  local copies, waits for them, and re-layouts: 870 us -> 13.2 us
  waiting for transfers between devices: 587 us -> 169 us
  Pallas kernels: 0 us -> 138 us
  matrix products: 101 us -> 0 us
  other arithmetic: 57.7 us -> 10.2 us
    gather x5 -> x0, local copies, waits for them, and re-layouts: 781 us -> none  [the longest x2 768 us: local_layer(): band_bias = jnp.take(rel_bias, jnp.clip(rel_offs, 0, 2 * window), axis=1)]
    psum x4 -> x0, waiting for transfers between devices: 587 us -> none  [the longest x1 289 us: local_layer(): attn_proj = lax.psum(attn_part, 'tp')]
    all_gather x0 -> x5, waiting for transfers between devices: none -> 153 us  [the longest x1 123 us: local_layer(): packed = lax.all_gather(piece, ('batch', 'tp', 'sp'), axis=0, tiled=False)]
    pallas_call x0 -> x10, Pallas kernels: none -> 138 us  [the longest x4 73.7 us: mlp(): pl.pallas_call(functools.partial(mlp_kernel, n_tp), grid=(rows // tile,),...]
    dot_general x12 -> x0, matrix products: 101 us -> none  [the longest x1 15.5 us: local_layer(): jnp.einsum('chqk,ckhd->cqhd', (win_exp / soft_sum).astype(jnp.bfloat16),...]
    scatter x2 -> x0, local copies, waits for them, and re-layouts: 50.6 us -> none  [local_layer(): heads_out = win_out.at[slot_rows].set(glob_out, mode='drop')]
    reduce_sum x3, other arithmetic: 24.7 us -> 0.89 us  [the longest x1 0.83 us: local_layer(): mine = got.astype(F32).sum(axis=0).astype(BF16)]
  transfers between devices with their start and end apart: 6 -> 11, of which waited for: 3 -> 7; matrix products, arithmetic and copies ran while one was open for 51% -> 3% of each run, Pallas kernels for 0% -> 25%
where the time goes in v1:
time: 387 us; the launch traced here: 380 us
  waiting for transfers between devices  169 us (44%)
  Pallas kernels  138 us (36%)
  starting transfers between devices  20.2 us (5%)
  blocking collectives  15.9 us (4%)
  between operations  13.6 us (4%)
  local copies, waits for them, and re-layouts  13.2 us (3%)
  other arithmetic  10.2 us (3%)
    all_gather x1, waiting for transfers between devices, local_layer(): packed = lax.all_gather(piece, ('batch', 'tp', 'sp'), axis=0, tiled=False)  123 us
    pallas_call x4, Pallas kernels, mlp(): pl.pallas_call(functools.partial(mlp_kernel, n_tp), grid=(rows // tile,),...  73.7 us
    pallas_call x4, Pallas kernels, window_attn(): pl.pallas_call(functools.partial(window_kernel, window, head_dim, chunk *...  39.5 us
    all_gather x4, waiting for transfers between devices, local_layer(): o_all = lax.all_gather(o, 'tp', axis=0)  30.3 us
    all_to_all x4, waiting for transfers between devices, spread(): return lax.all_to_all(part, 'sp', 0, 0)  16.1 us
    all_to_all x1, blocking collectives, spread(): return lax.all_to_all(part, 'sp', 0, 0)  15.9 us
    all_to_all x4, starting transfers between devices, spread(): return lax.all_to_all(part, 'sp', 0, 0)  15.5 us
    pallas_call x1, Pallas kernels, project(): pl.pallas_call(functools.partial(project_kernel, scale), grid=(rows // BL...  13 us
  transfers between devices with their start and end apart: 11, of which 7 were waited for; matrix products, arithmetic and copies ran while one was open for 3% of the time, Pallas kernels for 25%

profile of v1, /device:TPU:0, one launch (start us, length us, event | category | flops | bytes accessed | tf_op | source)
XLA Modules:
  0.0 380.1 jit_solution(6465369953741829042)
XLA Ops:
  8.2 13.0 %project.1 = (bf16[2048,256]{1,0:T(8,128)(2,1)}, bf16[2048,256]{1,0:T(8,128)(2,1)}, bf16[2048,256]{1,0:T(8,128)(2,1)}, bf16[512,768]{1,0:T(8,128)(2,1)}) custom-call(s32[512,1]{1,0:T(8,128)} %copy.16.slot_ref, bf16[2048,1024]{1,0:T(8,128)(2,1)} %x_ref.9, bf16[1024,256]{1,0:T(8,128)(2,1)} %wq_ref.1, bf16[1024,256]{1,0:T(8,128)(2,1)} %wk_ref.1, ...), custom_call_target="tpu_custom_call" | custom-call | flops 4294967296 | bytes 8388608 | tf_op jit(solution)/shard_map/project/pallas_call | solution.py:65
  21.2 15.9 %all_to_all.25 = bf16[4,128,768]{2,1,0:T(8,128)(2,1)S(1)} all-to-all(bf16[4,128,768]{2,1,0:T(8,128)(2,1)} %bitcast.67), channel_id=1, replica_groups=mesh['batch'=2,'tp'=4,'sp'=4] {'sp'}, dimensions={0} | all-to-all | bytes 1572864 | tf_op jit(solution)/shard_map/all_to_all | solution.py:270
  39.7 3.5 all-to-all-start.1
  49.7 4.9 %all-to-all-done.1 = bf16[4,128,768]{2,1,0:T(8,128)(2,1)S(1)} async-done(((bf16[4,128,768]{2,1,0:T(8,128)(2,1)}), bf16[4,128,768]{2,1,0:T(8,128)(2,1)S(1)}, u32[]{:S(2)}, u32[]{:S(2)}) %all-to-all-start.1) | async-done | bytes 786464 | tf_op jit(solution)/shard_map/all_to_all | solution.py:270
  55.5 11.8 %glob_partial.1 = (f32[512,256]{1,0:T(8,128)}, f32[512,256]{1,0:T(8,128)}) custom-call(bf16[512,768]{1,0:T(8,128)(2,1)} %bitcast.52, bf16[2048,256]{1,0:T(8,128)(2,1)} %get-tuple-element.12.k_ref, bf16[2048,256]{1,0:T(8,128)(2,1)} %get-tuple-element.13.v_ref), custom_call_target="tpu_custom_call" | custom-call | flops 1073741824 | bytes 2097152 | tf_op jit(solution)/shard_map/glob_partial/pallas_call | solution.py:102
  69.3 5.1 %all-to-all-start.3 = ((f32[4,128,2,2,2]{1,4,3,2,0:T(2,128)}), f32[4,128,2,2,2]{1,4,3,2,0:T(2,128)S(1)}, u32[]{:S(2)}, u32[]{:S(2)}) async-start(f32[4,128,2,2,2]{1,4,3,2,0:T(2,128)} %copy.19), calls=%async_computation.3 | async-start | bytes 32768 | tf_op jit(solution)/shard_map/all_to_all | solution.py:270
  78.1 3.5 all-to-all-start.2
  81.7 8.5 %all-to-all-done.2 = f32[4,128,256]{1,2,0:T(8,128)S(1)} async-done(((f32[4,128,256]{1,2,0:T(8,128)}), f32[4,128,256]{1,2,0:T(8,128)S(1)}, u32[]{:S(2)}, u32[]{:S(2)}) %all-to-all-start.2) | async-done | bytes 524320 | tf_op jit(solution)/shard_map/all_to_all | solution.py:270
  91.1 3.4 all-to-all-start.4
  94.6 3.0 pad_maximum_fusion.4
  97.5 2.7 all-to-all-done.4
  100.9 10.1 %window_attn.4 = bf16[512,256]{1,0:T(8,128)(2,1)} custom-call(s32[2]{0:T(128)} %add_convert_fusion.edge_ref, f32[4,1,1024]{2,1,0:T(1,128)} %broadcast_in_dim.10.bias_ref, s32[1,512]{1,0:T(1,128)} %bitcast.71, bf16[2048,256]{1,0:T(8,128)(2,1)} %get-tuple-element.11.q_ref, bf16[1024,256]{1,0:T(8,128)(2,1)} %get-tuple-element.36.kx_ref, ...), custom_call_target="tpu_custom_call" | custom-call | flops 671088640 | bytes 4194304 | tf_op jit(solution)/shard_map/window_attn/pallas_call | solution.py:175
  113.5 9.6 %window_attn.5 = bf16[512,256]{1,0:T(8,128)(2,1)} custom-call(s32[2]{0:T(128)} %add_convert_fusion.edge_ref, f32[4,1,1024]{2,1,0:T(1,128)} %broadcast_in_dim.10.bias_ref, s32[1,512]{1,0:T(1,128)} %bitcast.72, bf16[2048,256]{1,0:T(8,128)(2,1)} %get-tuple-element.11.q_ref, bf16[1024,256]{1,0:T(8,128)(2,1)} %get-tuple-element.34.kx_ref, ...), custom_call_target="tpu_custom_call" | custom-call | flops 671088640 | bytes 4194304 | tf_op jit(solution)/shard_map/window_attn/pallas_call | solution.py:175
  123.2 9.6 %window_attn.6 = bf16[512,256]{1,0:T(8,128)(2,1)} custom-call(s32[2]{0:T(128)} %add_convert_fusion.edge_ref, f32[4,1,1024]{2,1,0:T(1,128)} %broadcast_in_dim.10.bias_ref, s32[1,512]{1,0:T(1,128)} %bitcast.73, bf16[2048,256]{1,0:T(8,128)(2,1)} %get-tuple-element.11.q_ref, bf16[1024,256]{1,0:T(8,128)(2,1)} %get-tuple-element.35.kx_ref, ...), custom_call_target="tpu_custom_call" | custom-call | flops 671088640 | bytes 4194304 | tf_op jit(solution)/shard_map/window_attn/pallas_call | solution.py:175
  133.3 10.2 %window_attn.7 = bf16[512,256]{1,0:T(8,128)(2,1)} custom-call(s32[2]{0:T(128)} %add_convert_fusion.edge_ref, f32[4,1,1024]{2,1,0:T(1,128)} %broadcast_in_dim.10.bias_ref, s32[1,512]{1,0:T(1,128)} %bitcast.74, bf16[2048,256]{1,0:T(8,128)(2,1)} %get-tuple-element.11.q_ref, bf16[1024,256]{1,0:T(8,128)(2,1)} %get-tuple-element.33.kx_ref, ...), custom_call_target="tpu_custom_call" | custom-call | flops 671088640 | bytes 4194304 | tf_op jit(solution)/shard_map/window_attn/pallas_call | solution.py:175
  143.5 122.5 %all-gather.13.cloned.1.call-done = bf16[9216,1024]{1,0:T(8,128)(2,1)} async-done(((bf16[288,1024]{1,0:T(8,128)(2,1)}), bf16[9216,1024]{1,0:T(8,128)(2,1)}) %all-gather.13.cloned.1.call-update) | async-done | bytes 18874384 | tf_op jit(solution)/shard_map/all_gather | solution.py:264
  266.1 18.3 %mlp.4 = bf16[512,1024]{1,0:T(8,128)(2,1)} custom-call(bf16[4,512,256]{2,1,0:T(8,128)(2,1)} %bitcast.63, bf16[2048,1024]{1,0:T(8,128)(2,1)} %x_ref.9, bf16[2,4,4,288,1024]{4,3,2,1,0:T(8,128)(2,1)} %bitcast.40, bf16[2,4,4,288,1024]{4,3,2,1,0:T(8,128)(2,1)} %bitcast.41, bf16[2,4,4,288,1024]{4,3,2,1,0:T(8,128)(2,1)} %bitcast.42), custom_call_target="tpu_custom_call" | custom-call | flops 9663676416 | bytes 2097152 | tf_op jit(solution)/shard_map/mlp/pallas_call | solution.py:221
  284.3 9.7 %all-gather.15.cloned.1.call-done = bf16[2048,256]{1,0:T(8,128)(2,1)} async-done(((bf16[512,256]{1,0:T(8,128)(2,1)}), bf16[2048,256]{1,0:T(8,128)(2,1)}) %all-gather.15.cloned.1.call-update) | async-done | bytes 1048592 | tf_op jit(solution)/shard_map/all_gather | solution.py:302
  294.0 18.5 %mlp.5 = bf16[512,1024]{1,0:T(8,128)(2,1)} custom-call(bf16[4,512,256]{2,1,0:T(8,128)(2,1)} %bitcast.64, bf16[2048,1024]{1,0:T(8,128)(2,1)} %x_ref.9, bf16[2,4,4,288,1024]{4,3,2,1,0:T(8,128)(2,1)} %bitcast.43, bf16[2,4,4,288,1024]{4,3,2,1,0:T(8,128)(2,1)} %bitcast.44, bf16[2,4,4,288,1024]{4,3,2,1,0:T(8,128)(2,1)} %bitcast.45), custom_call_target="tpu_custom_call" | custom-call | flops 9663676416 | bytes 2097152 | tf_op jit(solution)/shard_map/mlp/pallas_call | solution.py:221
  312.5 10.2 %all-gather.17.cloned.1.call-done = bf16[2048,256]{1,0:T(8,128)(2,1)} async-done(((bf16[512,256]{1,0:T(8,128)(2,1)}), bf16[2048,256]{1,0:T(8,128)(2,1)}) %all-gather.17.cloned.1.call-update) | async-done | bytes 1048592 | tf_op jit(solution)/shard_map/all_gather | solution.py:302
  322.7 18.3 %mlp.6 = bf16[512,1024]{1,0:T(8,128)(2,1)} custom-call(bf16[4,512,256]{2,1,0:T(8,128)(2,1)} %bitcast.65, bf16[2048,1024]{1,0:T(8,128)(2,1)} %x_ref.9, bf16[2,4,4,288,1024]{4,3,2,1,0:T(8,128)(2,1)} %bitcast.46, bf16[2,4,4,288,1024]{4,3,2,1,0:T(8,128)(2,1)} %bitcast.47, bf16[2,4,4,288,1024]{4,3,2,1,0:T(8,128)(2,1)} %bitcast.48), custom_call_target="tpu_custom_call" | custom-call | flops 9663676416 | bytes 2097152 | tf_op jit(solution)/shard_map/mlp/pallas_call | solution.py:221
  341.0 10.4 %all-gather.19.cloned.1.call-done = bf16[2048,256]{1,0:T(8,128)(2,1)} async-done(((bf16[512,256]{1,0:T(8,128)(2,1)}), bf16[2048,256]{1,0:T(8,128)(2,1)}) %all-gather.19.cloned.1.call-update) | async-done | bytes 1048592 | tf_op jit(solution)/shard_map/all_gather | solution.py:302
  351.4 18.6 %mlp.7 = bf16[512,1024]{1,0:T(8,128)(2,1)} custom-call(bf16[4,512,256]{2,1,0:T(8,128)(2,1)} %bitcast.66, bf16[2048,1024]{1,0:T(8,128)(2,1)} %x_ref.9, bf16[2,4,4,288,1024]{4,3,2,1,0:T(8,128)(2,1)} %bitcast.49, bf16[2,4,4,288,1024]{4,3,2,1,0:T(8,128)(2,1)} %bitcast.50, bf16[2,4,4,288,1024]{4,3,2,1,0:T(8,128)(2,1)} %bitcast.51), custom_call_target="tpu_custom_call" | custom-call | flops 9663676416 | bytes 2097152 | tf_op jit(solution)/shard_map/mlp/pallas_call | solution.py:221
  370.1 3.3 pad_maximum_fusion
  (69 shorter events, 21.9 us)
Async XLA Ops:
  6.5 104.6 %copy-start = (bf16[256,1024]{1,0:T(8,128)(2,1)S(1)}, bf16[256,1024]{1,0:T(8,128)(2,1)}, u32[]{:S(2)}) copy-start(bf16[256,1024]{1,0:T(8,128)(2,1)} %param.17) | copy-start | bytes 1572868
  7.3 0.9 copy-start.11
  21.2 22.1 %copy-start.2 = (bf16[2048,256]{1,0:T(8,128)(2,1)S(1)}, bf16[2048,256]{1,0:T(8,128)(2,1)}, u32[]{:S(2)}) copy-start(bf16[2048,256]{1,0:T(8,128)(2,1)} %get-tuple-element.12.k_ref) | copy-start | bytes 3145732
  21.2 22.1 %copy-start.4 = (bf16[2048,256]{1,0:T(8,128)(2,1)S(1)}, bf16[2048,256]{1,0:T(8,128)(2,1)}, u32[]{:S(2)}) copy-start(bf16[2048,256]{1,0:T(8,128)(2,1)} %get-tuple-element.13.v_ref) | copy-start | bytes 3145732
  21.2 26.6 %copy-start.12 = (f32[4,513]{1,0:T(4,128)S(1)}, f32[4,513]{1,0:T(4,128)}, u32[]{:S(2)}) copy-start(f32[4,513]{1,0:T(4,128)} %param.12) | copy-start | bytes 24628
  39.7 14.9 %all-to-all-start.1 = ((bf16[4,128,768]{2,1,0:T(8,128)(2,1)}), bf16[4,128,768]{2,1,0:T(8,128)(2,1)S(1)}, u32[]{:S(2)}, u32[]{:S(2)}) async-start(bf16[4,128,768]{2,1,0:T(8,128)(2,1)} %broadcast_in_dim.13), calls=%async_computation.1 | async-start | bytes 1572864 | tf_op jit(solution)/shard_map/all_to_all | solution.py:270
  44.1 4.9 %collective-permute-start = (bf16[2,256,256]{2,1,0:T(8,128)(2,1)}, bf16[2,256,256]{2,1,0:T(8,128)(2,1)S(1)}, u32[]{:S(2)}, u32[]{:S(2)}) collective-permute-start(bf16[2,256,256]{2,1,0:T(8,128)(2,1)} %get-tuple-element.17), channel_id=1, source_target_pairs={{0,1},{1,2},{2,3},{4,5},{5,6},{6,7},{8,9},{9,10},{10,11},{12,13},{... | collective-permute-start | bytes 786440 | tf_op jit(solution)/shard_map/ppermute | solution.py:278
  46.5 27.9 %collective-permute-start.1 = (bf16[2,256,256]{2,1,0:T(8,128)(2,1)}, bf16[2,256,256]{2,1,0:T(8,128)(2,1)}, u32[]{:S(2)}, u32[]{:S(2)}) collective-permute-start(bf16[2,256,256]{2,1,0:T(8,128)(2,1)} %get-tuple-element.18), channel_id=1, source_target_pairs={{1,0},{2,1},{3,2},{5,4},{6,5},{7,6},{9,8},{10,9},{11,10},{13,12},{... | collective-permute-start | bytes 786440 | tf_op jit(solution)/shard_map/ppermute | solution.py:279
  54.6 0.9 copy-start.1
  55.5 39.0 %copy-start.3 = (bf16[2048,256]{1,0:T(8,128)(2,1)S(1)}, bf16[2048,256]{1,0:T(8,128)(2,1)}, u32[]{:S(2)}) copy-start(bf16[2048,256]{1,0:T(8,128)(2,1)} %get-tuple-element.12.k_ref) | copy-start | bytes 3145732
  55.5 39.0 %copy-start.5 = (bf16[2048,256]{1,0:T(8,128)(2,1)S(1)}, bf16[2048,256]{1,0:T(8,128)(2,1)}, u32[]{:S(2)}) copy-start(bf16[2048,256]{1,0:T(8,128)(2,1)} %get-tuple-element.13.v_ref) | copy-start | bytes 3145732
  67.3 27.2 %copy-start.10 = (bf16[256,256]{1,0:T(8,128)(2,1)S(1)}, bf16[256,256]{1,0:T(8,128)(2,1)}, u32[]{:S(2)}) copy-start(bf16[256,256]{1,0:T(8,128)(2,1)} %get-tuple-element.28) | copy-start | bytes 393220
  69.3 8.8 %all-to-all-start.3 = ((f32[4,128,2,2,2]{1,4,3,2,0:T(2,128)}), f32[4,128,2,2,2]{1,4,3,2,0:T(2,128)S(1)}, u32[]{:S(2)}, u32[]{:S(2)}) async-start(f32[4,128,2,2,2]{1,4,3,2,0:T(2,128)} %copy.19), calls=%async_computation.3 | async-start | bytes 32768 | tf_op jit(solution)/shard_map/all_to_all | solution.py:270
  78.1 12.0 %all-to-all-start.2 = ((f32[4,128,256]{1,2,0:T(8,128)}), f32[4,128,256]{1,2,0:T(8,128)S(1)}, u32[]{:S(2)}, u32[]{:S(2)}) async-start(f32[4,128,256]{1,2,0:T(8,128)} %copy.17), calls=%async_computation.2 | async-start | bytes 1048576 | tf_op jit(solution)/shard_map/all_to_all | solution.py:270
  91.1 9.2 %all-to-all-start.4 = ((bf16[4,128,256]{2,1,0:T(8,128)(2,1)}), bf16[4,128,256]{2,1,0:T(8,128)(2,1)S(1)}, u32[]{:S(2)}, u32[]{:S(2)}) async-start(bf16[4,128,256]{2,1,0:T(8,128)(2,1)} %broadcast_in_dim.14), calls=%async_computation.4 | async-start | bytes 524288 | tf_op jit(solution)/shard_map/all_to_all | solution.py:270
  94.5 49.1 %all-gather.11.cloned.1.call-start = ((), (), s32[]{:S(2)}) async-start(), calls=%async_computation.5 | async-start | bytes 1310720 | tf_op jit(solution)/shard_map/all_gather | solution.py:302
  100.2 0.7 copy-start.6
  111.1 155.0 %all-gather.13.cloned.1.call-start = ((), (), s32[]{:S(2)}) async-start(), calls=%async_computation.6 | async-start | bytes 19464192 | tf_op jit(solution)/shard_map/all_gather | solution.py:264
  113.2 180.9 %all-gather.15.cloned.1.call-start = ((), (), s32[]{:S(2)}) async-start(), calls=%async_computation.7 | async-start | bytes 1310720 | tf_op jit(solution)/shard_map/all_gather | solution.py:302
  123.1 199.6 %all-gather.17.cloned.1.call-start = ((), (), s32[]{:S(2)}) async-start(), calls=%async_computation.8 | async-start | bytes 1310720 | tf_op jit(solution)/shard_map/all_gather | solution.py:302
  132.8 218.7 %all-gather.19.cloned.1.call-start = ((), (), s32[]{:S(2)}) async-start(), calls=%async_computation.9 | async-start | bytes 1310720 | tf_op jit(solution)/shard_map/all_gather | solution.py:302
  351.4 18.7 %copy-start.7 = (bf16[512,1024]{1,0:T(8,128)(2,1)S(1)}, bf16[512,1024]{1,0:T(8,128)(2,1)}, u32[]{:S(2)}) copy-start(bf16[512,1024]{1,0:T(8,128)(2,1)} %mlp.4) | copy-start | bytes 3145732
  351.4 18.7 %copy-start.8 = (bf16[512,1024]{1,0:T(8,128)(2,1)S(1)}, bf16[512,1024]{1,0:T(8,128)(2,1)}, u32[]{:S(2)}) copy-start(bf16[512,1024]{1,0:T(8,128)(2,1)} %mlp.5) | copy-start | bytes 3145732
  351.4 18.7 %copy-start.9 = (bf16[512,1024]{1,0:T(8,128)(2,1)S(1)}, bf16[512,1024]{1,0:T(8,128)(2,1)}, u32[]{:S(2)}) copy-start(bf16[512,1024]{1,0:T(8,128)(2,1)} %mlp.6) | copy-start | bytes 3145732
Sparse Core Ops, SparseCore 0:
  111.2 28.8 all-gather.10
  143.0 122.9 all-gather.12
  267.6 26.3 all-gather.14
  295.4 27.2 all-gather.16
  324.1 27.2 all-gather.18

commit v2 on v0

v2 whole, which is shorter than its diff:
```python
import functools

import jax
import jax.numpy as jnp
from jax import lax
from jax.experimental import pallas as pl
from jax.experimental.pallas import tpu as pltpu
from jax.sharding import PartitionSpec as P

BLK = 256
F32 = jnp.float32
BF16 = jnp.bfloat16
MESH = pl.DeviceIdType.MESH
VMEM_CAP = 67043328


def dot_nn(a, b):
    return lax.dot_general(a, b, (((1,), (0,)), ((), ())), preferred_element_type=F32)


def dot_nt(a, b):
    return lax.dot_general(a, b, (((1,), (1,)), ((), ())), preferred_element_type=F32)


def layer_kernel(
    n_tp, n_seq, window, head_dim, heads,
    slot_col, slot_row, bias_ref, x_hbm, wq_hbm, wk_hbm, wv_hbm, wg_hbm, wu_hbm, wd_hbm, wo_hbm,
    out_hbm,
    x_ref, wq_ref, wk_ref, wv_ref, wg_ref, wbuf, q_ref, kvx, acc_ref, sel_ref, sel_r1, sel_s1, sel_r2, sel_all,
    band_ref, g_ref, g_r1, g_s1, g_r2, gout_ref, o_raw, o_all, stage,
    x_sem, w_sem, own_sem, out_sem, halo_s, halo_r, sel_s, sel_r, g_s, g_r,
    z_s, z_r, zr_s, a_s, a_r, b_s, b_r, c_s, c_r, o_s, o_r, or_s,
):
    rows, dim = x_ref.shape
    width = wq_ref.shape[1]
    num_glob = slot_col.shape[0]
    half = num_glob // 2
    blocks = rows // BLK
    span = bias_ref.shape[2]
    band_w = 3 * window
    pair = 2 * head_dim
    scale = head_dim ** -0.5
    up_rows = wu_hbm.shape[1]
    out_rows = wo_hbm.shape[1]
    piece_rows = 2 * up_rows + out_rows
    cut = piece_rows // 2

    b = lax.axis_index("batch")
    t = lax.axis_index("tp")
    s = lax.axis_index("sp")
    core = s % 2
    partner = {"sp": s + 1 - 2 * core}
    y_peer = {"sp": (s + 2) % 4}
    x_peer = {"batch": 1 - b}
    near = t + 1 - 2 * (t % 2)
    side = t // 2
    across = 2 - side
    far = 3 - 3 * side
    inner = (t == 1) | (t == 2)
    near_dev, across_dev = {"tp": near}, {"tp": across}
    srcs = (near, across, far)
    rep = b * n_seq + s
    rep_x = (1 - b) * n_seq + s
    rep_y = b * n_seq + (s + 2) % 4
    rep_d = (1 - b) * n_seq + (s + 2) % 4

    def remote(src, dst, ssem, rsem, dev):
        return pltpu.make_async_remote_copy(src_ref=src, dst_ref=dst, send_sem=ssem, recv_sem=rsem, device_id=dev, device_id_type=MESH)

    def load_x(i):
        at = pl.ds(pl.multiple_of(i * BLK, BLK), BLK)
        return pltpu.make_async_copy(x_hbm.at[at], x_ref.at[at], x_sem.at[i])

    own = [
        pltpu.make_async_copy(wu_hbm, wbuf.at[t, :, pl.ds(0, up_rows)], own_sem.at[0]),
        pltpu.make_async_copy(wd_hbm, wbuf.at[t, :, pl.ds(up_rows, up_rows)], own_sem.at[1]),
        pltpu.make_async_copy(wo_hbm, wbuf.at[t, :, pl.ds(2 * up_rows, out_rows)], own_sem.at[2]),
    ]
    wload = [pltpu.make_async_copy(h, v, w_sem.at[j]) for j, (h, v) in enumerate(((wk_hbm, wk_ref), (wv_hbm, wv_ref), (wg_hbm, wg_ref), (wq_hbm, wq_ref)))]
    for copy in own:
        copy.start()
    for copy in wload:
        copy.start()
    for i in range(blocks):
        load_x(i).start()

    barrier = pltpu.get_barrier_semaphore()
    peers = [{"tp": (t + d) % n_tp} for d in (1, 2, 3)] + [{"sp": (s + d) % n_seq} for d in (1, 2, 3)] + [x_peer]
    for dev in peers:
        pl.semaphore_signal(barrier, inc=1, device_id=dev, device_id_type=MESH)
    pl.semaphore_wait(barrier, len(peers))
    for copy in own:
        copy.wait()

    def piece(src, r):
        return wbuf.at[src, r]

    def z_copy(j):
        return remote(piece(t, rep), piece(t, rep), z_s.at[j], z_r.at[t], (near_dev, across_dev)[j])

    def z_wait(k):
        remote(piece(srcs[k], rep), piece(srcs[k], rep), z_s.at[0], z_r.at[srcs[k]], near_dev).wait_recv()

    def z_relay(k):
        return remote(piece(srcs[k], rep), piece(srcs[k], rep), zr_s.at[k - 1], z_r.at[srcs[k]], near_dev)

    def a_copy(k, j):
        return remote(piece(srcs[k], rep), piece(srcs[k], rep), a_s.at[k, j], a_r.at[k, j], (x_peer, y_peer, partner)[j])

    def a_wait(k, j):
        r = (rep_x, rep_y)[j]
        remote(piece(srcs[k], r), piece(srcs[k], r), a_s.at[k, j], a_r.at[k, j], (x_peer, y_peer)[j]).wait_recv()

    def b_copy(k, j):
        r = (rep_x, rep_y, rep_x, rep_y)[j]
        ref = piece(srcs[k], r)
        if j == 2:
            ref = wbuf.at[srcs[k], r, pl.ds(0, cut)]
        if j == 3:
            ref = wbuf.at[srcs[k], r, pl.ds(cut, cut)]
        return remote(ref, ref, b_s.at[k, j], b_r.at[k, j], (partner, partner, y_peer, x_peer)[j])

    def b_wait(k, j):
        ref = wbuf.at[srcs[k], rep_d, pl.ds(0 if j == 2 else cut, cut)]
        remote(ref, ref, b_s.at[k, j], b_r.at[k, j], partner).wait_recv()

    def c_copy(k):
        return remote(piece(srcs[k], rep_d), piece(srcs[k], rep_d), c_s.at[k], c_r.at[k], partner)

    def phase_a(k):
        for j in range(3):
            a_copy(k, j).start()

    def phase_b(k):
        a_wait(k, 0)
        b_copy(k, 2).start()
        b_copy(k, 0).start()
        a_wait(k, 1)
        b_copy(k, 3).start()
        b_copy(k, 1).start()

    def phase_c(k):
        b_wait(k, 2)
        b_wait(k, 3)
        c_copy(k).start()

    def weights_done():
        rp = (s + 1 - 2 * core)
        base, basex = b * n_seq, (1 - b) * n_seq
        for k in range(3):
            remote(piece(srcs[k], base + rp), piece(srcs[k], base + rp), a_s.at[k, 2], a_r.at[k, 2], partner).wait_recv()
            remote(piece(srcs[k], basex + rp), piece(srcs[k], basex + rp), b_s.at[k, 0], b_r.at[k, 0], partner).wait_recv()
            ry = (rp + 2) % 4
            remote(piece(srcs[k], base + ry), piece(srcs[k], base + ry), b_s.at[k, 1], b_r.at[k, 1], partner).wait_recv()
            remote(piece(srcs[k], basex + ry), piece(srcs[k], basex + ry), c_s.at[k], c_r.at[k], partner).wait_recv()

    z_copy(0).start()
    z_copy(1).start()

    acc_ref[...] = jnp.zeros_like(acc_ref)
    for copy in wload[:3]:
        copy.wait()

    def project(i, carry):
        load_x(i).wait()
        at = pl.ds(pl.multiple_of(i * BLK, BLK), BLK)
        x = x_ref[at, :]
        k = dot_nn(x, wk_ref[...]).astype(BF16)
        v = dot_nn(x, wv_ref[...]).astype(BF16)
        qg = dot_nn(x, wg_ref[...]).astype(BF16) * scale
        ext = pl.ds(pl.multiple_of(i * BLK + window, BLK), BLK)
        kvx[ext, :width] = k
        kvx[ext, width:] = v
        cols = lax.broadcasted_iota(jnp.int32, (num_glob, BLK), 1) + i * BLK
        pick = jnp.where(slot_col[...] == cols, 1.0, 0.0).astype(BF16)
        acc_ref[:, :width] += dot_nn(pick, qg)
        acc_ref[:, width:2 * width] += dot_nn(pick, k)
        acc_ref[:, 2 * width:] += dot_nn(pick, v)
        return carry

    lax.fori_loop(0, blocks, project, 0)
    sel_ref[...] = acc_ref[...].astype(BF16)

    mine = pl.ds(pl.multiple_of(core * half, half), half)
    theirs = pl.ds(pl.multiple_of((1 - core) * half, half), half)

    def swap(ref, r1, s1, r2, full, ssem, rsem):
        first = remote(ref.at[theirs], r1, ssem.at[0], rsem.at[0], partner)
        second = remote(s1, r2, ssem.at[1], rsem.at[1], y_peer)
        third = remote(full.at[mine], full.at[mine], ssem.at[2], rsem.at[2], partner)
        third_in = remote(full.at[theirs], full.at[theirs], ssem.at[2], rsem.at[2], partner)
        return first, second, third, third_in

    sel1, sel2, sel3, sel3_in = swap(sel_ref, sel_r1, sel_s1, sel_r2, sel_all, sel_s, sel_r)
    sel1.start()
    edge = (pl.ds(window, window), pl.ds(rows, window))
    halo_left = remote(kvx.at[edge[0]], kvx.at[pl.ds(rows + window, window)], halo_s.at[0], halo_r.at[0], {"sp": (s + 3) % n_seq})
    halo_right = remote(kvx.at[edge[1]], kvx.at[pl.ds(0, window)], halo_s.at[1], halo_r.at[1], {"sp": (s + 1) % n_seq})
    sel1.wait_recv()
    sel_s1[...] = sel_ref[mine, :] + sel_r1[...]
    sel2.start()
    halo_left.start()
    halo_right.start()

    z_wait(0)
    phase_a(0)

    @pl.when(inner)
    def _():
        z_wait(1)
        z_relay(1).start()

    wload[3].wait()

    def project_q(i, carry):
        at = pl.ds(pl.multiple_of(i * BLK, BLK), BLK)
        q_ref[at, :] = dot_nn(x_ref[at, :], wq_ref[...]).astype(BF16) * scale
        return carry

    lax.fori_loop(0, blocks, project_q, 0)

    cols = lax.broadcasted_iota(jnp.int32, (BLK, band_w), 1)

    def make_band(lo, hi):
        for h in range(heads):
            row = jnp.broadcast_to(bias_ref[h], (BLK, span))
            band = pltpu.roll(row, 0, 1, stride=1, stride_axis=0)[:, :band_w]
            band_ref[h] = jnp.where((cols >= lo) & (cols < hi), band, -jnp.inf)

    is_first = 1 - (s + n_seq - 1) // n_seq
    is_last = s // (n_seq - 1)
    make_band(window * is_first, band_w)

    sel2.wait_recv()
    sel_all[mine, :] = sel_s1[...] + sel_r2[...]
    sel3.start()

    @pl.when(jnp.logical_not(inner))
    def _():
        z_wait(1)

    phase_a(1)

    @pl.when(inner)
    def _():
        z_wait(2)
        z_relay(2).start()

    sel3_in.wait_recv()

    lane_p = lax.broadcasted_iota(jnp.int32, (1, pair), 1)
    low = lane_p < head_dim
    zero = jnp.zeros((), BF16)
    tile = 128

    def masked(xv, odd):
        return jnp.where(low, zero, xv) if odd else jnp.where(low, xv, zero)

    def glob(i, carry):
        at = pl.ds(pl.multiple_of(i * tile, tile), tile)
        lane = lax.broadcasted_iota(jnp.int32, (tile, 128), 1)
        stat = jnp.zeros((tile, 128), F32)
        for p in range(heads // 2):
            qg = sel_all[at, p * pair:(p + 1) * pair]
            k = kvx[pl.ds(window, rows), p * pair:(p + 1) * pair]
            v = kvx[pl.ds(window, rows), width + p * pair:width + (p + 1) * pair]
            outs = []
            for odd in (0, 1):
                sc = dot_nt(masked(qg, odd), k)
                m = jnp.max(sc, axis=1, keepdims=True)
                e = jnp.exp(sc - m)
                stat = jnp.where(lane == 2 * p + odd, m, stat)
                stat = jnp.where(lane == heads + 2 * p + odd, jnp.sum(e, axis=1, keepdims=True), stat)
                outs.append(dot_nn(e.astype(BF16), v))
            g_ref[at, p * pair:(p + 1) * pair] = jnp.where(low, outs[0], outs[1])
        g_ref[at, width:] = stat
        return carry

    lax.fori_loop(0, num_glob // tile, glob, 0)

    def merge(a, c):
        sa, sc = a[:, width:], c[:, width:]
        lane = lax.broadcasted_iota(jnp.int32, sa.shape, 1)
        wide = lax.broadcasted_iota(jnp.int32, (1, width), 1)
        fa = jnp.zeros((sa.shape[0], width), F32)
        fc, total = fa, fa
        stat = jnp.zeros_like(sa)
        for h in range(heads):
            ma, mc = sa[:, h:h + 1], sc[:, h:h + 1]
            la, lc = sa[:, heads + h:heads + h + 1], sc[:, heads + h:heads + h + 1]
            m = jnp.maximum(ma, mc)
            ea, ec = jnp.exp(ma - m), jnp.exp(mc - m)
            l = la * ea + lc * ec
            here = (wide >= h * head_dim) & (wide < (h + 1) * head_dim)
            fa = jnp.where(here, ea, fa)
            fc = jnp.where(here, ec, fc)
            total = jnp.where(here, l, total)
            stat = jnp.where(lane == h, m, stat)
            stat = jnp.where(lane == heads + h, l, stat)
        return a[:, :width] * fa + c[:, :width] * fc, total, stat

    g1, g2, g3, g3_in = swap(g_ref, g_r1, g_s1, g_r2, gout_ref, g_s, g_r)
    g1.start()
    halo_left.wait_recv()
    halo_right.wait_recv()

    slot = slot_row[...]
    lane_b = lax.broadcasted_iota(jnp.int32, (BLK, pair), 1)
    row_iota = lax.broadcasted_iota(jnp.int32, (BLK, num_glob), 0)

    def attend(i):
        dist = slot - i * BLK - row_iota
        near_by = jnp.abs(dist) <= window
        start = pl.multiple_of(i * BLK, BLK)
        for p in range(heads // 2):
            at = slice(p * pair, (p + 1) * pair)
            q = q_ref[pl.ds(start, BLK), at]
            k_win = kvx[pl.ds(start, band_w), at]
            v_win = kvx[pl.ds(start, band_w), width + p * pair:width + (p + 1) * pair]
            k_glob = sel_all[:, width + p * pair:width + (p + 1) * pair]
            v_glob = sel_all[:, 2 * width + p * pair:2 * width + (p + 1) * pair]
            outs = []
            for odd in (0, 1):
                qh = masked(q, odd)
                s_win = dot_nt(qh, k_win) + band_ref[2 * p + odd]
                s_glob = jnp.where(near_by, -jnp.inf, dot_nt(qh, k_glob))
                m = jnp.maximum(jnp.max(s_win, axis=1, keepdims=True), jnp.max(s_glob, axis=1, keepdims=True))
                e_win = jnp.exp(s_win - m)
                e_glob = jnp.exp(s_glob - m)
                inv = 1.0 / (jnp.sum(e_win, axis=1, keepdims=True) + jnp.sum(e_glob, axis=1, keepdims=True))
                o = dot_nn((e_win * inv).astype(BF16), v_win)
                outs.append(o + dot_nn((e_glob * inv).astype(BF16), v_glob))
            o_raw[pl.ds(start, BLK), at] = jnp.where(low, outs[0], outs[1]).astype(BF16)

    def block_ref(src, j):
        return o_all.at[src, pl.ds(pl.multiple_of(j * BLK, BLK), BLK)]

    def o_copy(j, way):
        return remote(block_ref(t, j), block_ref(t, j), o_s.at[way, j], o_r.at[t, j], (near_dev, across_dev)[way])

    def o_wait(src, j):
        remote(block_ref(src, j), block_ref(src, j), o_s.at[0, 0], o_r.at[src, j], near_dev).wait_recv()

    def o_relay(k, j):
        return remote(block_ref(srcs[k], j), block_ref(srcs[k], j), or_s.at[k - 1, j], o_r.at[srcs[k], j], near_dev)

    def finish(j, carry):
        at = pl.ds(pl.multiple_of(j * BLK, BLK), BLK)
        pick = jnp.where(slot - j * BLK == row_iota, 1.0, 0.0)
        is_glob = jnp.max(pick, axis=1, keepdims=True) > 0.0
        ins = dot_nn(pick.astype(BF16), gout_ref[...])
        o_all[t, at, :] = jnp.where(is_glob, ins, o_raw[at, :].astype(F32)).astype(BF16)
        o_copy(j, 0).start()
        o_copy(j, 1).start()
        return carry

    def relay(j, carry):
        for k in (1, 2):
            o_wait(srcs[k], j)
            o_relay(k, j).start()
        return carry

    def relays(lo, hi):
        @pl.when(inner)
        def _():
            lax.fori_loop(lo, hi, relay, 0)

    lag = 3

    def window_step(i, carry):
        attend(i)

        @pl.when(i == 0)
        def _():
            make_band(0, band_w)
            g1.wait_recv()
            num, total, stat = merge(g_ref[mine, :], g_r1[...])
            g_s1[:, :width] = num
            g_s1[:, width:] = stat
            g2.start()

            @pl.when(jnp.logical_not(inner))
            def _():
                z_wait(2)

            phase_b(0)
            phase_a(2)

        @pl.when(i == 2)
        def _():
            g2.wait_recv()
            num, total, stat = merge(g_s1[...], g_r2[...])
            gout_ref[mine, :] = (num / total).astype(BF16)
            g3.start()
            phase_b(1)

        @pl.when(i == 4)
        def _():
            phase_b(2)
            phase_c(0)

        @pl.when(i == 6)
        def _():
            make_band(0, band_w - window * is_last)
            phase_c(1)

        @pl.when(i == lag)
        def _():
            g3_in.wait_recv()
            lax.fori_loop(0, lag, finish, 0)

        @pl.when(i >= lag)
        def _():
            finish(i, 0)

        @pl.when(i == 5)
        def _():
            relays(0, 1)

        @pl.when(i == 6)
        def _():
            relays(1, 2)

        @pl.when(i == 7)
        def _():
            relays(2, 4)

        return carry

    lax.fori_loop(0, blocks, window_step, 0)
    phase_c(2)
    weights_done()

    def out_copy(i):
        return pltpu.make_async_copy(stage.at[i % 2], out_hbm.at[pl.ds(pl.multiple_of(i * BLK, BLK), BLK)], out_sem.at[i % 2])

    def mlp(i, carry):
        at = pl.ds(pl.multiple_of(i * BLK, BLK), BLK)
        o_wait(near, i)

        @pl.when(jnp.logical_not(inner))
        def _():
            o_wait(across, i)
            o_wait(far, i)

        acc = x_ref[at, :].astype(F32)
        for j in range(n_tp):
            acc += dot_nn(o_all[j, at, :], wbuf[j, :, 2 * up_rows:, :].reshape(width, dim))
        hidden = acc.astype(BF16)
        acc = hidden.astype(F32)
        for j in range(n_tp):
            up = dot_nn(hidden, wbuf[j, :, :up_rows, :].reshape(dim, dim))
            acc += dot_nn(jax.nn.gelu(up).astype(BF16), wbuf[j, :, up_rows:2 * up_rows, :].reshape(dim, dim))

        @pl.when(i >= 2)
        def _():
            out_copy(i - 2).wait()

        stage[i % 2] = acc.astype(BF16)
        out_copy(i).start()

        @pl.when(i == 0)
        def _():
            relays(4, 6)

        @pl.when(i == 1)
        def _():
            relays(6, 7)

        @pl.when(i == 2)
        def _():
            relays(7, 8)

        return carry

    lax.fori_loop(0, blocks, mlp, 0)

    out_copy(blocks - 2).wait()
    out_copy(blocks - 1).wait()
    for copy in (halo_left, halo_right, sel1, sel2, sel3, g1, g2, g3, z_copy(0), z_copy(1)):
        copy.wait_send()
    for k in range(3):
        for j in range(3):
            a_copy(k, j).wait_send()
        for j in range(4):
            b_copy(k, j).wait_send()
        c_copy(k).wait_send()

    def drain(j, carry):
        o_copy(j, 0).wait_send()
        o_copy(j, 1).wait_send()
        return carry

    lax.fori_loop(0, blocks, drain, 0)

    @pl.when(inner)
    def _():
        z_relay(1).wait_send()
        z_relay(2).wait_send()

        def drain_relay(j, carry):
            o_relay(1, j).wait_send()
            o_relay(2, j).wait_send()
            return carry

        lax.fori_loop(0, blocks, drain_relay, 0)


def solution(mesh):
    n_seq = mesh.shape["sp"]
    n_tp = mesh.shape["tp"]
    n_batch = mesh.shape["batch"]
    n_rep = n_seq * n_batch

    def local_layer(tokens, glob_pos, rel_bias, w_query, w_key, w_value, w_query_glob, w_out, w_up, w_down):
        rows, dim = tokens.shape
        heads = rel_bias.shape[0]
        window = (rel_bias.shape[1] - 1) // 2
        width = w_query.shape[1]
        head_dim = width // heads
        num_glob = glob_pos.shape[0]
        half = num_glob // 2
        slot = glob_pos - lax.axis_index("sp") * rows
        span = 4 * window
        bias = jnp.pad(rel_bias, ((0, 0), (0, span - rel_bias.shape[1])), constant_values=-jnp.inf)[:, None]
        blocks = rows // BLK
        up_rows, out_rows = dim // n_rep, width // n_rep
        stat_w = width + 128
        any_spec = pl.BlockSpec(memory_space=pl.ANY)
        vmem_spec = pl.BlockSpec(memory_space=pltpu.VMEM)
        dma = pltpu.SemaphoreType.DMA
        return pl.pallas_call(
            functools.partial(layer_kernel, n_tp, n_seq, window, head_dim, heads),
            out_shape=jax.ShapeDtypeStruct((rows, dim), BF16),
            in_specs=[vmem_spec] * 3 + [any_spec] * 8,
            out_specs=any_spec,
            scratch_shapes=[
                pltpu.VMEM((rows, dim), BF16),
                pltpu.VMEM((dim, width), BF16),
                pltpu.VMEM((dim, width), BF16),
                pltpu.VMEM((dim, width), BF16),
                pltpu.VMEM((dim, width), BF16),
                pltpu.VMEM((n_tp, n_rep, 2 * up_rows + out_rows, dim), BF16),
                pltpu.VMEM((rows, width), BF16),
                pltpu.VMEM((rows + 2 * window, 2 * width), BF16),
                pltpu.VMEM((num_glob, 3 * width), F32),
                pltpu.VMEM((num_glob, 3 * width), BF16),
                pltpu.VMEM((half, 3 * width), BF16),
                pltpu.VMEM((half, 3 * width), BF16),
                pltpu.VMEM((half, 3 * width), BF16),
                pltpu.VMEM((num_glob, 3 * width), BF16),
                pltpu.VMEM((heads, BLK, 3 * window), F32),
                pltpu.VMEM((num_glob, stat_w), F32),
                pltpu.VMEM((half, stat_w), F32),
                pltpu.VMEM((half, stat_w), F32),
                pltpu.VMEM((half, stat_w), F32),
                pltpu.VMEM((num_glob, width), BF16),
                pltpu.VMEM((rows, width), BF16),
                pltpu.VMEM((n_tp, rows, width), BF16),
                pltpu.VMEM((2, BLK, dim), BF16),
                dma((blocks,)), dma((4,)), dma((3,)), dma((2,)),
                dma((2,)), dma((2,)), dma((3,)), dma((3,)), dma((3,)), dma((3,)),
                dma((2,)), dma((n_tp,)), dma((2,)),
                dma((3, 3)), dma((3, 3)), dma((3, 4)), dma((3, 4)), dma((3,)), dma((3,)),
                dma((2, blocks)), dma((n_tp, blocks)), dma((2, blocks)),
            ],
            compiler_params=pltpu.CompilerParams(vmem_limit_bytes=VMEM_CAP, collective_id=0, has_side_effects=True),
            name="layer",
        )(
            slot[:, None], slot[None], bias, tokens, w_query, w_key, w_value, w_query_glob,
            w_up.reshape(n_rep, up_rows, dim), w_down.reshape(n_rep, up_rows, dim), w_out.reshape(n_rep, out_rows, dim),
        )

    row_spec = P(("batch", "sp"), None)
    col_spec = P(None, "tp")
    head_spec = P("tp", None)
    in_specs = (row_spec, P("batch"), head_spec, col_spec, col_spec, col_spec, col_spec, head_spec, col_spec, head_spec)
    return jax.shard_map(local_layer, mesh=mesh, in_specs=in_specs, out_specs=row_spec, check_vma=False)
```

time: 1670 us -> 161 us (0.10); the launches traced: 1650 us -> 161 us
  local copies, waits for them, and re-layouts: 870 us -> 6.82 us
  waiting for transfers between devices: 587 us -> 0 us
  Pallas kernels: 0 us -> 153 us
  matrix products: 101 us -> 0 us
  other arithmetic: 57.7 us -> 0.68 us
    gather x5 -> x0, local copies, waits for them, and re-layouts: 781 us -> none  [the longest x2 768 us: local_layer(): band_bias = jnp.take(rel_bias, jnp.clip(rel_offs, 0, 2 * window), axis=1)]
    psum x4 -> x0, waiting for transfers between devices: 587 us -> none  [the longest x1 289 us: local_layer(): attn_proj = lax.psum(attn_part, 'tp')]
    pallas_call x0 -> x1, Pallas kernels: none -> 153 us  [local_layer(): pl.pallas_call(functools.partial(layer_kernel, n_tp, n_seq, window, head_...]
    dot_general x12 -> x0, matrix products: 101 us -> none  [the longest x1 15.5 us: local_layer(): jnp.einsum('chqk,ckhd->cqhd', (win_exp / soft_sum).astype(jnp.bfloat16),...]
    scatter x2 -> x0, local copies, waits for them, and re-layouts: 50.6 us -> none  [local_layer(): heads_out = win_out.at[slot_rows].set(glob_out, mode='drop')]
    reduce_sum x3 -> x0, other arithmetic: 24.7 us -> none  [the longest x1 8.65 us: local_layer(): glob_exp.sum(axis=-1, keepdims=True)]
  transfers between devices with their start and end apart: 6 -> 0, of which waited for: 3 -> 0; matrix products, arithmetic and copies ran while one was open for 51% -> 0% of each run, Pallas kernels for 0% -> 0%
where the time goes in v2:
time: 161 us
  Pallas kernels  153 us (95%)
  local copies, waits for them, and re-layouts  6.82 us (4%)
    pallas_call x1, Pallas kernels, local_layer(): pl.pallas_call(functools.partial(layer_kernel, n_tp, n_seq, window, head_...  153 us
    unnamed x3, local copies, waits for them, and re-layouts  4.64 us

profile of v2, /device:TPU:0, one launch (start us, length us, event | category | flops | bytes accessed | tf_op | source)
XLA Modules:
  0.0 160.8 jit_solution(15866697325710059242)
XLA Ops:
  0.0 0.7 broadcast_subtract_fusion
  0.7 0.0 copy-start
  0.7 0.7 pad.4
  1.4 0.6 broadcast_in_dim.11.bias_ref
  2.0 0.0 copy-done
  2.0 0.9 copy.11.slot_col
  2.9 153.3 %layer.1 = bf16[2048,1024]{1,0:T(8,128)(2,1)} custom-call(s32[512,1]{1,0:T(8,128)} %copy.11.slot_col, s32[1,512]{1,0:T(1,128)} %bitcast.9, f32[4,1,1024]{2,1,0:T(1,128)} %broadcast_in_dim.11.bias_ref, bf16[2048,1024]{1,0:T(8,128)(2,1)} %x_hbm.1, bf16[1024,256]{1,0:T(8,128)(2,1)} %wq_hbm.1, bf16[1024,256]{1,0:T(8,128)(2,1)} %wk_hbm.1, ...), custom_call_target="tpu_custom_call" | custom-call | tf_op jit(solution)/shard_map/layer/pallas_call | solution.py:532
  156.2 4.6 %copy.13 = bf16[2048,1024]{1,0:T(8,128)(2,1)} copy(bf16[2048,1024]{1,0:T(8,128)(2,1)} %layer.1) | data formatting | bytes 8388608
Async XLA Ops:
  0.7 1.3 copy-start

commit v3 on v2

--- a/solution.py
+++ b/solution.py
@@ -26,9 +26,9 @@
     n_tp, n_seq, window, head_dim, heads,
     slot_col, slot_row, bias_ref, x_hbm, wq_hbm, wk_hbm, wv_hbm, wg_hbm, wu_hbm, wd_hbm, wo_hbm,
     out_hbm,
-    x_ref, wq_ref, wk_ref, wv_ref, wg_ref, wbuf, q_ref, kvx, acc_ref, sel_ref, sel_r1, sel_s1, sel_r2, sel_all,
+    x_ref, wq_ref, wk_ref, wv_ref, wg_ref, wbuf, q_ref, kvx, acc_ref, qsel_ref, qsel_r1, qsel_s1, qsel_r2, qsel_all, sel_ref, sel_r1, sel_s1, sel_r2, sel_all,
     band_ref, g_ref, g_r1, g_s1, g_r2, gout_ref, o_raw, o_all, stage,
-    x_sem, w_sem, own_sem, out_sem, halo_s, halo_r, sel_s, sel_r, g_s, g_r,
+    x_sem, w_sem, own_sem, out_sem, halo_s, halo_r, qsel_s, qsel_r, sel_s, sel_r, g_s, g_r,
     z_s, z_r, zr_s, a_s, a_r, b_s, b_r, c_s, c_r, o_s, o_r, or_s,
 ):
     rows, dim = x_ref.shape
@@ -42,8 +42,8 @@
     scale = head_dim ** -0.5
     up_rows = wu_hbm.shape[1]
     out_rows = wo_hbm.shape[1]
-    piece_rows = 2 * up_rows + out_rows
-    cut = piece_rows // 2
+    part_rows = (2 * up_rows + out_rows) // 2
+    cut = part_rows // 3
 
     b = lax.axis_index("batch")
     t = lax.axis_index("tp")
@@ -92,94 +92,83 @@
     for copy in own:
         copy.wait()
 
-    def piece(src, r):
-        return wbuf.at[src, r]
-
-    def z_copy(j):
-        return remote(piece(t, rep), piece(t, rep), z_s.at[j], z_r.at[t], (near_dev, across_dev)[j])
-
-    def z_wait(k):
-        remote(piece(srcs[k], rep), piece(srcs[k], rep), z_s.at[0], z_r.at[srcs[k]], near_dev).wait_recv()
-
-    def z_relay(k):
-        return remote(piece(srcs[k], rep), piece(srcs[k], rep), zr_s.at[k - 1], z_r.at[srcs[k]], near_dev)
-
-    def a_copy(k, j):
-        return remote(piece(srcs[k], rep), piece(srcs[k], rep), a_s.at[k, j], a_r.at[k, j], (x_peer, y_peer, partner)[j])
-
-    def a_wait(k, j):
-        r = (rep_x, rep_y)[j]
-        remote(piece(srcs[k], r), piece(srcs[k], r), a_s.at[k, j], a_r.at[k, j], (x_peer, y_peer)[j]).wait_recv()
-
-    def b_copy(k, j):
+    def piece(src, r, c, lo=0, size=part_rows):
+        return wbuf.at[src, r, pl.ds(c * part_rows + lo, size)]
+
+    def z_copy(j, c):
+        ref = piece(t, rep, c)
+        return remote(ref, ref, z_s.at[j, c], z_r.at[t, c], (near_dev, across_dev)[j])
+
+    def z_wait(k, c):
+        ref = piece(srcs[k], rep, c)
+        remote(ref, ref, z_s.at[0, c], z_r.at[srcs[k], c], near_dev).wait_recv()
+
+    def z_relay(k, c):
+        ref = piece(srcs[k], rep, c)
+        return remote(ref, ref, zr_s.at[k - 1, c], z_r.at[srcs[k], c], near_dev)
+
+    def relay_weights(k, c):
+        @pl.when(inner)
+        def _():
+            z_wait(k, c)
+            z_relay(k, c).start()
+
+    def end_wait(k, c):
+        @pl.when(jnp.logical_not(inner))
+        def _():
+            z_wait(k, c)
+
+    def a_copy(k, c, j):
+        ref = piece(srcs[k], rep, c)
+        return remote(ref, ref, a_s.at[k, c, j], a_r.at[k, c, j], (x_peer, y_peer, partner)[j])
+
+    def a_start(k, c, *ways):
+        for j in ways:
+            a_copy(k, c, j).start()
+
+    def a_wait(k, c, j):
+        ref = piece(srcs[k], (rep_x, rep_y)[j], c)
+        remote(ref, ref, a_s.at[k, c, j], a_r.at[k, c, j], (x_peer, y_peer)[j]).wait_recv()
+
+    def b_copy(k, c, j):
         r = (rep_x, rep_y, rep_x, rep_y)[j]
-        ref = piece(srcs[k], r)
-        if j == 2:
-            ref = wbuf.at[srcs[k], r, pl.ds(0, cut)]
-        if j == 3:
-            ref = wbuf.at[srcs[k], r, pl.ds(cut, cut)]
-        return remote(ref, ref, b_s.at[k, j], b_r.at[k, j], (partner, partner, y_peer, x_peer)[j])
-
-    def b_wait(k, j):
-        ref = wbuf.at[srcs[k], rep_d, pl.ds(0 if j == 2 else cut, cut)]
-        remote(ref, ref, b_s.at[k, j], b_r.at[k, j], partner).wait_recv()
-
-    def c_copy(k):
-        return remote(piece(srcs[k], rep_d), piece(srcs[k], rep_d), c_s.at[k], c_r.at[k], partner)
-
-    def phase_a(k):
-        for j in range(3):
-            a_copy(k, j).start()
-
-    def phase_b(k):
-        a_wait(k, 0)
-        b_copy(k, 2).start()
-        b_copy(k, 0).start()
-        a_wait(k, 1)
-        b_copy(k, 3).start()
-        b_copy(k, 1).start()
-
-    def phase_c(k):
-        b_wait(k, 2)
-        b_wait(k, 3)
-        c_copy(k).start()
+        ref = (piece(srcs[k], r, c), piece(srcs[k], r, c), piece(srcs[k], r, c, 0, cut), piece(srcs[k], r, c, cut, part_rows - cut))[j]
+        return remote(ref, ref, b_s.at[k, c, j], b_r.at[k, c, j], (partner, partner, y_peer, x_peer)[j])
+
+    def phase_b(k, c):
+        a_wait(k, c, 1)
+        b_copy(k, c, 3).start()
+        b_copy(k, c, 1).start()
+        a_wait(k, c, 0)
+        b_copy(k, c, 2).start()
+        b_copy(k, c, 0).start()
+
+    def c_copy(k, c):
+        ref = piece(srcs[k], rep_d, c)
+        return remote(ref, ref, c_s.at[k, c], c_r.at[k, c], partner)
+
+    def phase_c(k, c):
+        for j, ref in ((2, piece(srcs[k], rep_d, c, 0, cut)), (3, piece(srcs[k], rep_d, c, cut, part_rows - cut))):
+            remote(ref, ref, b_s.at[k, c, j], b_r.at[k, c, j], partner).wait_recv()
+        c_copy(k, c).start()
 
     def weights_done():
-        rp = (s + 1 - 2 * core)
-        base, basex = b * n_seq, (1 - b) * n_seq
+        rp = s + 1 - 2 * core
+        ry = (rp + 2) % 4
+        base, base_x = b * n_seq, (1 - b) * n_seq
         for k in range(3):
-            remote(piece(srcs[k], base + rp), piece(srcs[k], base + rp), a_s.at[k, 2], a_r.at[k, 2], partner).wait_recv()
-            remote(piece(srcs[k], basex + rp), piece(srcs[k], basex + rp), b_s.at[k, 0], b_r.at[k, 0], partner).wait_recv()
-            ry = (rp + 2) % 4
-            remote(piece(srcs[k], base + ry), piece(srcs[k], base + ry), b_s.at[k, 1], b_r.at[k, 1], partner).wait_recv()
-            remote(piece(srcs[k], basex + ry), piece(srcs[k], basex + ry), c_s.at[k], c_r.at[k], partner).wait_recv()
-
-    z_copy(0).start()
-    z_copy(1).start()
-
-    acc_ref[...] = jnp.zeros_like(acc_ref)
-    for copy in wload[:3]:
-        copy.wait()
-
-    def project(i, carry):
-        load_x(i).wait()
-        at = pl.ds(pl.multiple_of(i * BLK, BLK), BLK)
-        x = x_ref[at, :]
-        k = dot_nn(x, wk_ref[...]).astype(BF16)
-        v = dot_nn(x, wv_ref[...]).astype(BF16)
-        qg = dot_nn(x, wg_ref[...]).astype(BF16) * scale
-        ext = pl.ds(pl.multiple_of(i * BLK + window, BLK), BLK)
-        kvx[ext, :width] = k
-        kvx[ext, width:] = v
-        cols = lax.broadcasted_iota(jnp.int32, (num_glob, BLK), 1) + i * BLK
-        pick = jnp.where(slot_col[...] == cols, 1.0, 0.0).astype(BF16)
-        acc_ref[:, :width] += dot_nn(pick, qg)
-        acc_ref[:, width:2 * width] += dot_nn(pick, k)
-        acc_ref[:, 2 * width:] += dot_nn(pick, v)
-        return carry
-
-    lax.fori_loop(0, blocks, project, 0)
-    sel_ref[...] = acc_ref[...].astype(BF16)
+            for c in range(2):
+                for ref, ssem, rsem in (
+                    (piece(srcs[k], base + rp, c), a_s.at[k, c, 2], a_r.at[k, c, 2]),
+                    (piece(srcs[k], base_x + rp, c), b_s.at[k, c, 0], b_r.at[k, c, 0]),
+                    (piece(srcs[k], base + ry, c), b_s.at[k, c, 1], b_r.at[k, c, 1]),
+                    (piece(srcs[k], base_x + ry, c), c_s.at[k, c], c_r.at[k, c]),
+                ):
+                    remote(ref, ref, ssem, rsem, partner).wait_recv()
+
+    for j in range(2):
+        for c in range(2):
+            z_copy(j, c).start()
 
     mine = pl.ds(pl.multiple_of(core * half, half), half)
     theirs = pl.ds(pl.multiple_of((1 - core) * half, half), half)
@@ -191,62 +180,85 @@
         third_in = remote(full.at[theirs], full.at[theirs], ssem.at[2], rsem.at[2], partner)
         return first, second, third, third_in
 
+    qs1, qs2, qs3, qs3_in = swap(qsel_ref, qsel_r1, qsel_s1, qsel_r2, qsel_all, qsel_s, qsel_r)
     sel1, sel2, sel3, sel3_in = swap(sel_ref, sel_r1, sel_s1, sel_r2, sel_all, sel_s, sel_r)
+
+    def pick_cols(i):
+        cols = lax.broadcasted_iota(jnp.int32, (num_glob, BLK), 1) + i * BLK
+        return jnp.where(slot_col[...] == cols, 1.0, 0.0).astype(BF16)
+
+    acc_ref[...] = jnp.zeros_like(acc_ref)
+    wload[2].wait()
+
+    def project_g(i, carry):
+        load_x(i).wait()
+        at = pl.ds(pl.multiple_of(i * BLK, BLK), BLK)
+        qg = dot_nn(x_ref[at, :], wg_ref[...]).astype(BF16) * scale
+        acc_ref[:, 2 * width:] += dot_nn(pick_cols(i), qg)
+        return carry
+
+    lax.fori_loop(0, blocks, project_g, 0)
+    qsel_ref[...] = acc_ref[:, 2 * width:].astype(BF16)
+    qs1.start()
+    wload[0].wait()
+    wload[1].wait()
+
+    def project(i, carry):
+        at = pl.ds(pl.multiple_of(i * BLK, BLK), BLK)
+        x = x_ref[at, :]
+        k = dot_nn(x, wk_ref[...]).astype(BF16)
+        v = dot_nn(x, wv_ref[...]).astype(BF16)
+        ext = pl.ds(pl.multiple_of(i * BLK + window, BLK), BLK)
+        kvx[ext, :width] = k
+        kvx[ext, width:] = v
+        pick = pick_cols(i)
+        acc_ref[:, :width] += dot_nn(pick, k)
+        acc_ref[:, width:2 * width] += dot_nn(pick, v)
+
+        @pl.when(i == 1)
+        def _():
+            qs1.wait_recv()
+            qsel_s1[...] = qsel_ref[mine, :] + qsel_r1[...]
+            qs2.start()
+            relay_weights(1, 0)
+            z_wait(0, 0)
+            a_start(0, 0, 0, 1, 2)
+
+        @pl.when(i == 6)
+        def _():
+            qs2.wait_recv()
+            qsel_all[mine, :] = qsel_s1[...] + qsel_r2[...]
+            qs3.start()
+
+        return carry
+
+    lax.fori_loop(0, blocks, project, 0)
+    sel_ref[...] = acc_ref[:, :2 * width].astype(BF16)
     sel1.start()
-    edge = (pl.ds(window, window), pl.ds(rows, window))
-    halo_left = remote(kvx.at[edge[0]], kvx.at[pl.ds(rows + window, window)], halo_s.at[0], halo_r.at[0], {"sp": (s + 3) % n_seq})
-    halo_right = remote(kvx.at[edge[1]], kvx.at[pl.ds(0, window)], halo_s.at[1], halo_r.at[1], {"sp": (s + 1) % n_seq})
-    sel1.wait_recv()
-    sel_s1[...] = sel_ref[mine, :] + sel_r1[...]
-    sel2.start()
-    halo_left.start()
-    halo_right.start()
-
-    z_wait(0)
-    phase_a(0)
-
-    @pl.when(inner)
-    def _():
-        z_wait(1)
-        z_relay(1).start()
-
-    wload[3].wait()
-
-    def project_q(i, carry):
-        at = pl.ds(pl.multiple_of(i * BLK, BLK), BLK)
-        q_ref[at, :] = dot_nn(x_ref[at, :], wq_ref[...]).astype(BF16) * scale
-        return carry
-
-    lax.fori_loop(0, blocks, project_q, 0)
-
-    cols = lax.broadcasted_iota(jnp.int32, (BLK, band_w), 1)
-
-    def make_band(lo, hi):
-        for h in range(heads):
-            row = jnp.broadcast_to(bias_ref[h], (BLK, span))
-            band = pltpu.roll(row, 0, 1, stride=1, stride_axis=0)[:, :band_w]
-            band_ref[h] = jnp.where((cols >= lo) & (cols < hi), band, -jnp.inf)
-
-    is_first = 1 - (s + n_seq - 1) // n_seq
-    is_last = s // (n_seq - 1)
-    make_band(window * is_first, band_w)
-
-    sel2.wait_recv()
-    sel_all[mine, :] = sel_s1[...] + sel_r2[...]
-    sel3.start()
-
-    @pl.when(jnp.logical_not(inner))
-    def _():
-        z_wait(1)
-
-    phase_a(1)
-
-    @pl.when(inner)
-    def _():
-        z_wait(2)
-        z_relay(2).start()
-
-    sel3_in.wait_recv()
+    halo_left = remote(kvx.at[pl.ds(window, window)], kvx.at[pl.ds(rows + window, window)], halo_s.at[0], halo_r.at[0], {"sp": (s + 3) % n_seq})
+    halo_right = remote(kvx.at[pl.ds(rows, window)], kvx.at[pl.ds(0, window)], halo_s.at[1], halo_r.at[1], {"sp": (s + 1) % n_seq})
+    has_left, has_right = s > 0, s < n_seq - 1
+    relay_weights(1, 1)
+
+    @pl.when(has_left)
+    def _():
+        halo_left.start()
+
+    @pl.when(has_right)
+    def _():
+        halo_right.start()
+
+    @pl.when(jnp.logical_not(has_left))
+    def _():
+        kvx[pl.ds(0, window), :] = jnp.zeros((window, 2 * width), BF16)
+
+    @pl.when(jnp.logical_not(has_right))
+    def _():
+        kvx[pl.ds(rows + window, window), :] = jnp.zeros((window, 2 * width), BF16)
+
+    z_wait(0, 1)
+    a_start(0, 1, 0, 1, 2)
+    qs3_in.wait_recv()
 
     lane_p = lax.broadcasted_iota(jnp.int32, (1, pair), 1)
     low = lane_p < head_dim
@@ -261,7 +273,7 @@
         lane = lax.broadcasted_iota(jnp.int32, (tile, 128), 1)
         stat = jnp.zeros((tile, 128), F32)
         for p in range(heads // 2):
-            qg = sel_all[at, p * pair:(p + 1) * pair]
+            qg = qsel_all[at, p * pair:(p + 1) * pair]
             k = kvx[pl.ds(window, rows), p * pair:(p + 1) * pair]
             v = kvx[pl.ds(window, rows), width + p * pair:width + (p + 1) * pair]
             outs = []
@@ -274,6 +286,18 @@
                 outs.append(dot_nn(e.astype(BF16), v))
             g_ref[at, p * pair:(p + 1) * pair] = jnp.where(low, outs[0], outs[1])
         g_ref[at, width:] = stat
+
+        @pl.when(i == 0)
+        def _():
+            sel1.wait_recv()
+            sel_s1[...] = sel_ref[mine, :] + sel_r1[...]
+            sel2.start()
+
+        @pl.when(i == 2)
+        def _():
+            end_wait(1, 0)
+            a_start(1, 0, 0, 2)
+
         return carry
 
     lax.fori_loop(0, num_glob // tile, glob, 0)
@@ -301,8 +325,54 @@
 
     g1, g2, g3, g3_in = swap(g_ref, g_r1, g_s1, g_r2, gout_ref, g_s, g_r)
     g1.start()
-    halo_left.wait_recv()
-    halo_right.wait_recv()
+    sel2.wait_recv()
+    sel_all[mine, :] = sel_s1[...] + sel_r2[...]
+    sel3.start()
+
+    wload[3].wait()
+
+    def project_q(i, carry):
+        at = pl.ds(pl.multiple_of(i * BLK, BLK), BLK)
+        q_ref[at, :] = dot_nn(x_ref[at, :], wq_ref[...]).astype(BF16) * scale
+
+        @pl.when(i == 2)
+        def _():
+            g1.wait_recv()
+            num, total, stat = merge(g_ref[mine, :], g_r1[...])
+            g_s1[:, :width] = num
+            g_s1[:, width:] = stat
+            g2.start()
+            a_start(1, 0, 1)
+            relay_weights(2, 0)
+            phase_b(0, 0)
+
+        return carry
+
+    lax.fori_loop(0, blocks, project_q, 0)
+
+    cols = lax.broadcasted_iota(jnp.int32, (BLK, band_w), 1)
+
+    def make_band(lo, hi):
+        for h in range(heads):
+            row = jnp.broadcast_to(bias_ref[h], (BLK, span))
+            band = pltpu.roll(row, 0, 1, stride=1, stride_axis=0)[:, :band_w]
+            band_ref[h] = jnp.where((cols >= lo) & (cols < hi), band, -jnp.inf)
+
+    is_first = 1 - (s + n_seq - 1) // n_seq
+    is_last = s // (n_seq - 1)
+    make_band(window * is_first, band_w)
+    end_wait(1, 1)
+    a_start(1, 1, 0, 1, 2)
+
+    @pl.when(has_left)
+    def _():
+        halo_right.wait_recv()
+
+    @pl.when(has_right)
+    def _():
+        halo_left.wait_recv()
+
+    sel3_in.wait_recv()
 
     slot = slot_row[...]
     lane_b = lax.broadcasted_iota(jnp.int32, (BLK, pair), 1)
@@ -317,8 +387,8 @@
             q = q_ref[pl.ds(start, BLK), at]
             k_win = kvx[pl.ds(start, band_w), at]
             v_win = kvx[pl.ds(start, band_w), width + p * pair:width + (p + 1) * pair]
-            k_glob = sel_all[:, width + p * pair:width + (p + 1) * pair]
-            v_glob = sel_all[:, 2 * width + p * pair:2 * width + (p + 1) * pair]
+            k_glob = sel_all[:, p * pair:(p + 1) * pair]
+            v_glob = sel_all[:, width + p * pair:width + (p + 1) * pair]
             outs = []
             for odd in (0, 1):
                 qh = masked(q, odd)
@@ -365,7 +435,7 @@
         def _():
             lax.fori_loop(lo, hi, relay, 0)
 
-    lag = 3
+    lag = 2
 
     def window_step(i, carry):
         attend(i)
@@ -373,36 +443,44 @@
         @pl.when(i == 0)
         def _():
             make_band(0, band_w)
-            g1.wait_recv()
-            num, total, stat = merge(g_ref[mine, :], g_r1[...])
-            g_s1[:, :width] = num
-            g_s1[:, width:] = stat
-            g2.start()
-
-            @pl.when(jnp.logical_not(inner))
-            def _():
-                z_wait(2)
-
-            phase_b(0)
-            phase_a(2)
-
-        @pl.when(i == 2)
+            relay_weights(2, 1)
+            phase_b(0, 1)
+
+        @pl.when(i == 1)
         def _():
             g2.wait_recv()
             num, total, stat = merge(g_s1[...], g_r2[...])
             gout_ref[mine, :] = (num / total).astype(BF16)
             g3.start()
-            phase_b(1)
+
+        @pl.when(i == 2)
+        def _():
+            phase_b(1, 0)
+
+        @pl.when(i == 3)
+        def _():
+            end_wait(2, 0)
+            a_start(2, 0, 0, 1, 2)
+            phase_c(0, 0)
 
         @pl.when(i == 4)
         def _():
-            phase_b(2)
-            phase_c(0)
+            phase_b(1, 1)
+
+        @pl.when(i == 5)
+        def _():
+            end_wait(2, 1)
+            a_start(2, 1, 0, 1, 2)
+            phase_c(0, 1)
 
         @pl.when(i == 6)
         def _():
             make_band(0, band_w - window * is_last)
-            phase_c(1)
+
+        @pl.when(i == 7)
+        def _():
+            phase_b(2, 0)
+            phase_c(1, 0)
 
         @pl.when(i == lag)
         def _():
@@ -413,22 +491,18 @@
         def _():
             finish(i, 0)
 
-        @pl.when(i == 5)
-        def _():
-            relays(0, 1)
-
-        @pl.when(i == 6)
-        def _():
-            relays(1, 2)
-
-        @pl.when(i == 7)
-        def _():
-            relays(2, 4)
+        @pl.when(i >= 4)
+        def _():
+            relays(i - 4, i - 3)
 
         return carry
 
     lax.fori_loop(0, blocks, window_step, 0)
-    phase_c(2)
+    phase_c(1, 1)
+    phase_b(2, 1)
+    phase_c(2, 0)
+    relays(4, 5)
+    phase_c(2, 1)
     weights_done()
 
     def out_copy(i):
@@ -461,15 +535,11 @@
 
         @pl.when(i == 0)
         def _():
-            relays(4, 6)
+            relays(5, 6)
 
         @pl.when(i == 1)
         def _():
-            relays(6, 7)
-
-        @pl.when(i == 2)
-        def _():
-            relays(7, 8)
+            relays(6, 8)
 
         return carry
 
@@ -477,14 +547,25 @@
 
     out_copy(blocks - 2).wait()
     out_copy(blocks - 1).wait()
-    for copy in (halo_left, halo_right, sel1, sel2, sel3, g1, g2, g3, z_copy(0), z_copy(1)):
+    @pl.when(has_left)
+    def _():
+        halo_left.wait_send()
+
+    @pl.when(has_right)
+    def _():
+        halo_right.wait_send()
+
+    for copy in (qs1, qs2, qs3, sel1, sel2, sel3, g1, g2, g3):
         copy.wait_send()
-    for k in range(3):
-        for j in range(3):
-            a_copy(k, j).wait_send()
-        for j in range(4):
-            b_copy(k, j).wait_send()
-        c_copy(k).wait_send()
+    for c in range(2):
+        z_copy(0, c).wait_send()
+        z_copy(1, c).wait_send()
+        for k in range(3):
+            for j in range(3):
+                a_copy(k, c, j).wait_send()
+            for j in range(4):
+                b_copy(k, c, j).wait_send()
+            c_copy(k, c).wait_send()
 
     def drain(j, carry):
         o_copy(j, 0).wait_send()
@@ -495,8 +576,9 @@
 
     @pl.when(inner)
     def _():
-        z_relay(1).wait_send()
-        z_relay(2).wait_send()
+        for k in (1, 2):
+            for c in range(2):
+                z_relay(k, c).wait_send()
 
         def drain_relay(j, carry):
             o_relay(1, j).wait_send()
@@ -544,11 +626,8 @@
                 pltpu.VMEM((rows, width), BF16),
                 pltpu.VMEM((rows + 2 * window, 2 * width), BF16),
                 pltpu.VMEM((num_glob, 3 * width), F32),
-                pltpu.VMEM((num_glob, 3 * width), BF16),
-                pltpu.VMEM((half, 3 * width), BF16),
-                pltpu.VMEM((half, 3 * width), BF16),
-                pltpu.VMEM((half, 3 * width), BF16),
-                pltpu.VMEM((num_glob, 3 * width), BF16),
+                *[pltpu.VMEM((n, width), BF16) for n in (num_glob, half, half, half, num_glob)],
+                *[pltpu.VMEM((n, 2 * width), BF16) for n in (num_glob, half, half, half, num_glob)],
                 pltpu.VMEM((heads, BLK, 3 * window), F32),
                 pltpu.VMEM((num_glob, stat_w), F32),
                 pltpu.VMEM((half, stat_w), F32),
@@ -559,9 +638,9 @@
                 pltpu.VMEM((n_tp, rows, width), BF16),
                 pltpu.VMEM((2, BLK, dim), BF16),
                 dma((blocks,)), dma((4,)), dma((3,)), dma((2,)),
-                dma((2,)), dma((2,)), dma((3,)), dma((3,)), dma((3,)), dma((3,)),
-                dma((2,)), dma((n_tp,)), dma((2,)),
-                dma((3, 3)), dma((3, 3)), dma((3, 4)), dma((3, 4)), dma((3,)), dma((3,)),
+                dma((2,)), dma((2,)), *[dma((3,))] * 6,
+                dma((2, 2)), dma((n_tp, 2)), dma((2, 2)),
+                dma((3, 2, 3)), dma((3, 2, 3)), dma((3, 2, 4)), dma((3, 2, 4)), dma((3, 2)), dma((3, 2)),
                 dma((2, blocks)), dma((n_tp, blocks)), dma((2, blocks)),
             ],
             compiler_params=pltpu.CompilerParams(vmem_limit_bytes=VMEM_CAP, collective_id=0, has_side_effects=True),

time: 161 us -> 149 us (0.925)
  the two profiles are of different devices: /device:TPU:0 before, /device:TPU:17 now
where the time goes in v3:
time: 149 us
  Pallas kernels  141 us (95%)
  local copies, waits for them, and re-layouts  6.82 us (5%)
    pallas_call x1, Pallas kernels, local_layer(): pl.pallas_call(functools.partial(layer_kernel, n_tp, n_seq, window, head_...  141 us
    unnamed x3, local copies, waits for them, and re-layouts  4.64 us

profile of v3, /device:TPU:17, one launch (start us, length us, event | category | flops | bytes accessed | tf_op | source)
XLA Modules:
  0.0 148.8 jit_solution(7952011115449474528)
XLA Ops:
  0.0 0.7 broadcast_subtract_fusion
  0.7 0.0 copy-start
  0.7 0.7 pad.4
  1.4 0.6 broadcast_in_dim.11.bias_ref
  2.0 0.0 copy-done
  2.0 0.9 copy.11.slot_col
  2.9 141.3 %layer.1 = bf16[2048,1024]{1,0:T(8,128)(2,1)} custom-call(s32[512,1]{1,0:T(8,128)} %copy.11.slot_col, s32[1,512]{1,0:T(1,128)} %bitcast.9, f32[4,1,1024]{2,1,0:T(1,128)} %broadcast_in_dim.11.bias_ref, bf16[2048,1024]{1,0:T(8,128)(2,1)} %x_hbm.1, bf16[1024,256]{1,0:T(8,128)(2,1)} %wq_hbm.1, bf16[1024,256]{1,0:T(8,128)(2,1)} %wk_hbm.1, ...), custom_call_target="tpu_custom_call" | custom-call | tf_op jit(solution)/shard_map/layer/pallas_call | solution.py:614
  144.2 4.6 %copy.13 = bf16[2048,1024]{1,0:T(8,128)(2,1)} copy(bf16[2048,1024]{1,0:T(8,128)(2,1)} %layer.1) | data formatting | bytes 8388608
Async XLA Ops:
  0.7 1.3 copy-start

commit v4 on v3

--- a/solution.py
+++ b/solution.py
@@ -24,7 +24,7 @@
 
 def layer_kernel(
     n_tp, n_seq, window, head_dim, heads,
-    slot_col, slot_row, bias_ref, x_hbm, wq_hbm, wk_hbm, wv_hbm, wg_hbm, wu_hbm, wd_hbm, wo_hbm,
+    pos_ref, bias_ref, x_hbm, wq_hbm, wk_hbm, wv_hbm, wg_hbm, wu_hbm, wd_hbm, wo_hbm,
     out_hbm,
     x_ref, wq_ref, wk_ref, wv_ref, wg_ref, wbuf, q_ref, kvx, acc_ref, qsel_ref, qsel_r1, qsel_s1, qsel_r2, qsel_all, sel_ref, sel_r1, sel_s1, sel_r2, sel_all,
     band_ref, g_ref, g_r1, g_s1, g_r2, gout_ref, o_raw, o_all, stage,
@@ -33,10 +33,10 @@
 ):
     rows, dim = x_ref.shape
     width = wq_ref.shape[1]
-    num_glob = slot_col.shape[0]
+    num_glob = pos_ref.shape[1]
     half = num_glob // 2
     blocks = rows // BLK
-    span = bias_ref.shape[2]
+    span = bias_ref.shape[1]
     band_w = 3 * window
     pair = 2 * head_dim
     scale = head_dim ** -0.5
@@ -166,8 +166,8 @@
                 ):
                     remote(ref, ref, ssem, rsem, partner).wait_recv()
 
-    for j in range(2):
-        for c in range(2):
+    for c in range(2):
+        for j in range(2):
             z_copy(j, c).start()
 
     mine = pl.ds(pl.multiple_of(core * half, half), half)
@@ -183,9 +183,12 @@
     qs1, qs2, qs3, qs3_in = swap(qsel_ref, qsel_r1, qsel_s1, qsel_r2, qsel_all, qsel_s, qsel_r)
     sel1, sel2, sel3, sel3_in = swap(sel_ref, sel_r1, sel_s1, sel_r2, sel_all, sel_s, sel_r)
 
+    slot = pos_ref[...] - s * rows
+    slot_col = jnp.transpose(jnp.broadcast_to(slot, (8, num_glob)))[:, :1]
+
     def pick_cols(i):
         cols = lax.broadcasted_iota(jnp.int32, (num_glob, BLK), 1) + i * BLK
-        return jnp.where(slot_col[...] == cols, 1.0, 0.0).astype(BF16)
+        return jnp.where(slot_col == cols, 1.0, 0.0).astype(BF16)
 
     acc_ref[...] = jnp.zeros_like(acc_ref)
     wload[2].wait()
@@ -354,7 +357,7 @@
 
     def make_band(lo, hi):
         for h in range(heads):
-            row = jnp.broadcast_to(bias_ref[h], (BLK, span))
+            row = jnp.broadcast_to(bias_ref[h:h + 1, :], (BLK, span))
             band = pltpu.roll(row, 0, 1, stride=1, stride_axis=0)[:, :band_w]
             band_ref[h] = jnp.where((cols >= lo) & (cols < hi), band, -jnp.inf)
 
@@ -374,7 +377,6 @@
 
     sel3_in.wait_recv()
 
-    slot = slot_row[...]
     lane_b = lax.broadcasted_iota(jnp.int32, (BLK, pair), 1)
     row_iota = lax.broadcasted_iota(jnp.int32, (BLK, num_glob), 0)
 
@@ -491,9 +493,9 @@
         def _():
             finish(i, 0)
 
-        @pl.when(i >= 4)
-        def _():
-            relays(i - 4, i - 3)
+        @pl.when(i >= 6)
+        def _():
+            relays(i - 6, i - 5)
 
         return carry
 
@@ -501,8 +503,8 @@
     phase_c(1, 1)
     phase_b(2, 1)
     phase_c(2, 0)
-    relays(4, 5)
     phase_c(2, 1)
+    relays(2, 4)
     weights_done()
 
     def out_copy(i):
@@ -535,7 +537,7 @@
 
         @pl.when(i == 0)
         def _():
-            relays(5, 6)
+            relays(4, 6)
 
         @pl.when(i == 1)
         def _():
@@ -602,9 +604,8 @@
         head_dim = width // heads
         num_glob = glob_pos.shape[0]
         half = num_glob // 2
-        slot = glob_pos - lax.axis_index("sp") * rows
         span = 4 * window
-        bias = jnp.pad(rel_bias, ((0, 0), (0, span - rel_bias.shape[1])), constant_values=-jnp.inf)[:, None]
+        bias = jnp.pad(rel_bias, ((0, 0), (0, span - rel_bias.shape[1])), constant_values=-jnp.inf)
         blocks = rows // BLK
         up_rows, out_rows = dim // n_rep, width // n_rep
         stat_w = width + 128
@@ -614,7 +615,7 @@
         return pl.pallas_call(
             functools.partial(layer_kernel, n_tp, n_seq, window, head_dim, heads),
             out_shape=jax.ShapeDtypeStruct((rows, dim), BF16),
-            in_specs=[vmem_spec] * 3 + [any_spec] * 8,
+            in_specs=[vmem_spec] * 2 + [any_spec] * 8,
             out_specs=any_spec,
             scratch_shapes=[
                 pltpu.VMEM((rows, dim), BF16),
@@ -646,7 +647,7 @@
             compiler_params=pltpu.CompilerParams(vmem_limit_bytes=VMEM_CAP, collective_id=0, has_side_effects=True),
             name="layer",
         )(
-            slot[:, None], slot[None], bias, tokens, w_query, w_key, w_value, w_query_glob,
+            glob_pos[None], bias, tokens, w_query, w_key, w_value, w_query_glob,
             w_up.reshape(n_rep, up_rows, dim), w_down.reshape(n_rep, up_rows, dim), w_out.reshape(n_rep, out_rows, dim),
         )
 

time: 149 us -> 147 us (0.987)
  the two profiles are of different devices: /device:TPU:17 before, /device:TPU:0 now
where the time goes in v4:
time: 147 us; the launch traced here: 145 us
  Pallas kernels  139 us (95%)
  local copies, waits for them, and re-layouts  5.95 us (4%)
    pallas_call x1, Pallas kernels, local_layer(): pl.pallas_call(functools.partial(layer_kernel, n_tp, n_seq, window, head_...  139 us
    unnamed x1, local copies, waits for them, and re-layouts  4.64 us

profile of v4, /device:TPU:0, one launch (start us, length us, event | category | flops | bytes accessed | tf_op | source)
XLA Modules:
  0.0 145.4 jit_solution(15810186789151783353)
XLA Ops:
  0.0 1.3 pad.4.bias_ref
  1.3 139.4 %layer.1 = bf16[2048,1024]{1,0:T(8,128)(2,1)} custom-call(s32[1,512]{1,0:T(1,128)} %bitcast.7, f32[4,1024]{1,0:T(4,128)} %pad.4.bias_ref, bf16[2048,1024]{1,0:T(8,128)(2,1)} %x_hbm.1, bf16[1024,256]{1,0:T(8,128)(2,1)} %wq_hbm.1, bf16[1024,256]{1,0:T(8,128)(2,1)} %wk_hbm.1, bf16[1024,256]{1,0:T(8,128)(2,1)} %wv_hbm.1, bf16[1024,256]{1,0:T(8,128)(2,1)} %wg_hbm.1, ...), custom_call_target="tpu_custom_call" | custom-call | tf_op jit(solution)/shard_map/layer/pallas_call | solution.py:615
  140.7 4.6 %copy.12 = bf16[2048,1024]{1,0:T(8,128)(2,1)} copy(bf16[2048,1024]{1,0:T(8,128)(2,1)} %layer.1) | data formatting | bytes 8388608
